TPU v7x, 128 devices: a whole 4x4x4 slice. The times are simulated.
128 devices in a mesh: req: 2 (over core), seq: 64 (over x, z, y).
Axes of the slice: x: 4, y: 4, z: 4, core: 2. Of those that a mesh axis runs over, the one named last changes fastest.
Arguments:
- image_query: bfloat16 [1024, 1536], P(('req', 'seq')), parts along dimension 0, may hold values from -6 to 6
- image_key: bfloat16 [1024, 1536], P(('req', 'seq')), parts along dimension 0, may hold values from -6 to 6
- image_value: bfloat16 [1024, 1536], P(('req', 'seq')), parts along dimension 0, may hold values from -6 to 6
- text_query: bfloat16 [1024, 1536], P('req'), parts along dimension 0, may hold values from -6 to 6
- text_key: bfloat16 [1024, 1536], P('req'), parts along dimension 0, may hold values from -6 to 6
- text_value: bfloat16 [1024, 1536], P('req'), parts along dimension 0, may hold values from -6 to 6
- image_query_gain: float32 [128], replicated, may hold values from 1 to 8
- image_key_gain: float32 [128], replicated, may hold values from 1 to 8
- text_query_gain: float32 [128], replicated, may hold values from 1 to 2.5
- text_key_gain: float32 [128], replicated, may hold values from 1 to 2.5
- image_order: int32 [1024], P(('req', 'seq')), parts along dimension 0, may hold values from 0 to 511, each once
- text_length: int32 [2], P('req'), parts along dimension 0, may hold values from 256 to 512
Outputs:
- image_out: bfloat16 [1024, 1536], P(('req', 'seq')), parts along dimension 0
- text_out: bfloat16 [1024, 1536], P(('req', 'seq')), parts along dimension 0
There are 2 independent parts, one for each index of `req`. A program takes and returns all parts, laid end to end along the dimension named above; an argument that names none is the same for every part. Nothing has to cross between parts.
Inputs may be any that keep to these rules, and one draw needn't show every extreme that they name: `image_order`: every position 0 to 511 appears once.
All inputs are finite; a program needn't handle non-finite values.
Results may differ from a plain program's by a relative error of at most 0.005.
The roundings to bfloat16 on the way count: a program that leaves them out, or rounds other values in their place, can miss the bound.
Values may be sent and summed in bfloat16 or wider, within the bound.
No kernel may reach another device: no remote copies, remote signals or barrier semaphores. Data moves between devices by JAX's collectives and lax.ppermute only.
A program may use at most 64 MiB of HBM per device.

v0:
```python
import jax
import jax.numpy as jnp
from jax import lax
from jax.sharding import PartitionSpec as P

GRID_W = 64


epsilon = 1e-06
masked_score = -1e30


def in_one_piece(arrays, axis, dim, along):
    widths = [a.shape[along] for a in arrays]
    both = jnp.concatenate(arrays, axis=along)
    whole = lax.all_gather(both, axis, axis=dim, tiled=True)
    return tuple(jnp.split(whole, [sum(widths[:k]) for k in range(1, len(widths))], axis=along))


def head_norm(values, norm_gain, head_count):
    row_count = values.shape[0]
    shaped = values.astype(jnp.float32).reshape(row_count, head_count, -1)
    mean_square = jnp.mean(shaped * shaped, axis=-1, keepdims=True)
    return shaped * lax.rsqrt(mean_square + epsilon) * norm_gain


def rotate(normed, positions, half_length):
    row_count, head_count, head_dim = normed.shape
    pair_count = head_dim // 2
    pair_ids = jnp.arange(pair_count)
    first_axis = pair_ids < 8
    second = pair_ids < 36
    within = jnp.where(first_axis, pair_ids, jnp.where(second, pair_ids - 8, pair_ids - 36)).astype(
        jnp.float32
    )
    axis_dim = jnp.where(first_axis, 16.0, 56.0).astype(jnp.float32)
    frequency = jnp.power(jnp.float32(10000.0), -2.0 * within / axis_dim)
    image_index = positions // half_length
    inside = positions % half_length
    row_place = inside // GRID_W
    column_place = inside % GRID_W
    coordinate = jnp.where(
        first_axis[None, :],
        image_index[:, None],
        jnp.where(second[None, :], row_place[:, None], column_place[:, None]),
    ).astype(jnp.float32)
    angles = coordinate * frequency[None, :]
    cosine = jnp.cos(angles)[:, None, :]
    sine_part = jnp.sin(angles)[:, None, :]
    paired = normed.reshape(row_count, head_count, pair_count, 2)
    even_part = paired[..., 0]
    odd_part = paired[..., 1]
    turned = jnp.stack(
        [even_part * cosine - odd_part * sine_part, even_part * sine_part + odd_part * cosine],
        axis=-1,
    )
    return turned.reshape(row_count, head_count * head_dim)


def partial_attend(queries, key_block, value_block, key_mask, head_count):
    row_count = queries.shape[0]
    key_count = key_block.shape[0]
    query_heads = queries.reshape(row_count, head_count, -1)
    scaling = query_heads.shape[-1] ** (-0.5)
    scores = (
        jnp.einsum(
            "rhd,shd->rhs",
            query_heads,
            key_block.reshape(key_count, head_count, -1),
            preferred_element_type=jnp.float32,
        )
        * scaling
    )
    if key_mask is not None:
        scores = jnp.where(key_mask[None, None, :], scores, masked_score)
    row_max = jnp.max(scores, axis=-1)
    expo = jnp.exp(scores - row_max[..., None])
    if key_mask is not None:
        expo = jnp.where(key_mask[None, None, :], expo, 0.0)
    totals = jnp.sum(expo, axis=-1)
    blended = jnp.einsum(
        "rhs,shd->rhd",
        expo.astype(jnp.bfloat16),
        value_block.reshape(key_count, head_count, -1),
        preferred_element_type=jnp.float32,
    )
    return (row_max, totals, blended)


def combine(earlier, later):
    max_first, sum_first, out_first = earlier
    max_second, sum_second, out_second = later
    joint = jnp.maximum(max_first, max_second)
    factor_first = jnp.exp(max_first - joint)
    factor_second = jnp.exp(max_second - joint)
    return (
        joint,
        sum_first * factor_first + sum_second * factor_second,
        out_first * factor_first[..., None] + out_second * factor_second[..., None],
    )


def take_rows(state, begin, length):
    return jax.tree.map(lambda member: lax.dynamic_slice_in_dim(member, begin, length, 0), state)


def finish(state):
    row_max, totals, blended = state
    return (blended / totals[..., None]).reshape(blended.shape[0], -1).astype(jnp.bfloat16)


def local(
    image_query,
    image_key,
    image_value,
    text_query,
    text_key,
    text_value,
    image_query_gain,
    image_key_gain,
    text_query_gain,
    text_key_gain,
    image_order,
    text_length,
):
    head_size = image_query_gain.shape[0]
    head_count = image_query.shape[1] // head_size
    devices = lax.axis_size("seq")
    own_rows = image_query.shape[0]
    half_length = own_rows * devices // 2
    text_rows = text_query.shape[0]
    share = text_rows // devices
    first_row = lax.axis_index("seq") * share
    query_ready = rotate(
        head_norm(image_query, image_query_gain, head_count), image_order, half_length
    ).astype(jnp.bfloat16)
    key_ready = rotate(
        head_norm(image_key, image_key_gain, head_count), image_order, half_length
    ).astype(jnp.bfloat16)
    text_valid = jnp.arange(text_rows) < text_length[0]
    text_keys = (
        head_norm(text_key, text_key_gain, head_count).reshape(text_rows, -1).astype(jnp.bfloat16)
    )
    own_text = lax.dynamic_slice_in_dim(text_query, first_row, share, 0)
    own_ready = (
        head_norm(own_text, text_query_gain, head_count).reshape(share, -1).astype(jnp.bfloat16)
    )
    local_queries = jnp.concatenate([query_ready, own_ready], axis=0)
    text_state = partial_attend(local_queries, text_keys, text_value, text_valid, head_count)
    query_count = local_queries.shape[0]
    start_state = take_rows(text_state, 0, query_count)
    pieces = in_one_piece((key_ready, image_value), "seq", 0, 1)
    image_state = combine(
        start_state, partial_attend(local_queries, pieces[0], pieces[1], None, head_count)
    )
    image_out = finish(take_rows(image_state, 0, own_rows))
    text_out = finish(take_rows(image_state, own_rows, share))
    return (image_out, text_out)


def solution(mesh):
    placed = (
        P(("req", "seq"), None),
        P(("req", "seq"), None),
        P(("req", "seq"), None),
        P("req", None),
        P("req", None),
        P("req", None),
        P(),
        P(),
        P(),
        P(),
        P(("req", "seq")),
        P("req"),
    )
    return jax.shard_map(
        local,
        mesh=mesh,
        in_specs=placed,
        out_specs=(P(("req", "seq"), None), P(("req", "seq"), None)),
        check_vma=False,
    )
```

profile of v0, /device:TPU:0, one launch (start us, length us, event | category | flops | bytes accessed | tf_op | source)
XLA Modules:
  0.0 108.6 jit_solution(6413456446253419397)
XLA Ops:
  7.3 0.9 copy.65
  8.2 0.8 bitcast_reduce_fusion
  9.0 0.9 copy.53
  10.7 0.9 multiply_multiply_fusion
  11.6 3.2 %slice_multiply_fusion.1 = (f32[8,12,64,1]{0,3,2,1:T(1,128)S(1)}, f32[8,12,64,1]{0,3,2,1:T(1,128)S(1)}, f32[8,12,64,1]{0,3,2,1:T(1,128)S(1)}, f32[8,12,64,1]{0,3...) fusion(f32[8,12,64,2]{0,3,2,1:T(2,128)S(1)} %get-tuple-element., ...), kind=kLoop, calls=%fused_computation.23 | loop fusion | flops 49152 | bytes 299008 | tf_op jit(solution)/shard_map/mul | solution.py:54
  16.2 0.8 copy.71
  17.0 1.4 %pad_maximum_fusion.3 = bf16[8,3072]{1,0:T(8,128)(2,1)} fusion(bf16[8,1536]{1,0:T(8,128)(2,1)} %param.14, bf16[8,1536]{1,0:T(8,128)(2,1)} %copy.71), kind=kLoop, calls=%fused_computation.47 | loop fusion | flops 98304 | bytes 98304 | tf_op jit(solution)/shard_map/concatenate | solution.py:15
  20.0 0.7 copy.52
  21.3 1.7 %copy.63 = bf16[512,1536]{0,1:T(8,128)(2,1)S(1)} copy(bf16[512,1536]{1,0:T(8,128)(2,1)} %param.17) | data formatting | bytes 3145728 | tf_op args[5]
  23.0 2.1 %convert_multiply_fusion.1 = f32[512,1536]{0,1:T(8,128)} fusion(bf16[512,1536]{0,1:T(8,128)(2,1)S(1)} %copy.52), kind=kLoop, calls=%fused_computation.1 | loop fusion | flops 1572864 | bytes 4718592 | tf_op jit(solution)/shard_map/mul | solution.py:23
  25.2 2.3 %reduce_sum.54 = f32[512,12]{0,1:T(8,128)S(1)} reduce(f32[512,12,128]{0,2,1:T(8,128)} %bitcast.53, f32[]{:T(128)} %constant.75.clone.1), dimensions={2}, to_apply=%region_0.0 | reduce | flops 780288 | bytes 3170308 | tf_op jit(solution)/shard_map/reduce_sum | solution.py:23
  27.9 0.8 fusion.19
  28.8 0.8 fusion.24
  30.0 0.8 fusion.10
  30.8 57.3 %all-gather.2.cloned.1.call-done = bf16[512,3072]{1,0:T(8,128)(2,1)} async-done(((bf16[8,3072]{1,0:T(8,128)(2,1)}), bf16[512,3072]{1,0:T(8,128)(2,1)}) %all-gather.2.cloned.1.call-update) | async-done | bytes 3145744 | tf_op jit(solution)/shard_map/all_gather | solution.py:16
  88.1 3.8 %fusion.38 = (bf16[512,1536]{1,0:T(8,128)(2,1)}, bf16[512,1536]{1,0:T(8,128)(2,1)}) fusion(bf16[512,3072]{1,0:T(8,128)(2,1)} %all-gather.2.cloned.1.call-done), kind=kLoop, calls=%fused_computation.93 | loop fusion | bytes 6291456 | tf_op jit(solution)/shard_map/split | solution.py:17
  91.9 1.7 %copy.80 = bf16[512,1536]{0,1:T(8,128)(2,1)S(1)} copy(bf16[512,1536]{1,0:T(8,128)(2,1)} %get-tuple-element.10) | data formatting | bytes 3145728
  93.6 2.4 %fusion.40 = (f32[16,12]{0,1:T(8,128)}, f32[16,12,512]{2,0,1:T(8,128)}) fusion(bf16[512,12,128]{0,2,1:T(8,128)(2,1)S(1)} %bitcast.57, bf16[8,12,128]{2,0,1:T(8,128)(2,1)} %copy-done.4, bf16[8,12,128]{2,0,1:T(8,128)(2,1)} %copy-done.3), kind=kOutput, calls=%fused_computation.95 | convolution fusion | flops 25460544 | bytes 2016000 | tf_op jit(solution)/shard_map/rhd,shd->rhs/dot_general | solution.py:66
  96.0 1.7 %copy.81 = bf16[512,1536]{0,1:T(8,128)(2,1)S(1)} copy(bf16[512,1536]{1,0:T(8,128)(2,1)} %get-tuple-element.9) | data formatting | bytes 3145728
  97.8 1.3 %fusion.8 = f32[16,12]{0,1:T(8,128)S(1)} fusion(f32[16,12,512]{2,0,1:T(8,128)} %get-tuple-element.34, f32[16,12]{0,1:T(8,128)} %get-tuple-element.33), kind=kLoop, calls=%fused_computation.18 | loop fusion | flops 196416 | bytes 394752 | tf_op jit(solution)/shard_map/reduce_sum | solution.py:80
  99.0 0.7 multiply_add_fusion
  99.8 0.6 fusion.7
  100.4 0.6 fusion.6
  101.0 0.7 fusion.26
  (62 shorter events, 4.6 us)
Async XLA Ops:
  7.2 20.3 %copy-start = (f32[128]{0:T(128)S(1)}, f32[128]{0:T(128)}, u32[]{:S(2)}) copy-start(f32[128]{0:T(128)} %param.21) | copy-start | bytes 1540
  7.2 2.8 %copy-start.6 = (bf16[8,1536]{1,0:T(8,128)(2,1)S(1)}, bf16[8,1536]{1,0:T(8,128)(2,1)}, u32[]{:S(2)}) copy-start(bf16[8,1536]{1,0:T(8,128)(2,1)} %param.12) | copy-start | bytes 73732
  7.2 2.9 %copy-start.10 = (s32[8]{0:T(128)S(1)}, s32[8]{0:T(128)}, u32[]{:S(2)}) copy-start(s32[8]{0:T(128)} %param.22) | copy-start | bytes 100
  7.2 3.2 %copy-start.7 = (f32[128]{0:T(128)S(1)}, f32[128]{0:T(128)}, u32[]{:S(2)}) copy-start(f32[128]{0:T(128)} %param.18) | copy-start | bytes 1540
  7.2 3.3 %copy-start.8 = (f32[128]{0:T(128)S(1)}, f32[128]{0:T(128)}, u32[]{:S(2)}) copy-start(f32[128]{0:T(128)} %param.19) | copy-start | bytes 1540
  7.2 80.9 %all-gather.2.cloned.1.call-start = ((), (), s32[]{:S(2)}) async-start(), calls=%async_computation | async-start | bytes 3194880 | tf_op jit(solution)/shard_map/all_gather | solution.py:16
  16.2 3.7 %copy-start.2 = (bf16[512,1536]{1,0:T(8,128)(2,1)S(1)}, bf16[512,1536]{1,0:T(8,128)(2,1)}, u32[]{:S(2)}) copy-start(bf16[512,1536]{1,0:T(8,128)(2,1)} %param.16) | copy-start | bytes 4718596
  19.9 9.7 %copy-start.3 = (bf16[8,12,128]{2,0,1:T(8,128)(2,1)}, bf16[8,12,128]{2,0,1:T(8,128)(2,1)S(1)}, u32[]{:S(2)}) copy-start(bf16[8,12,128]{2,0,1:T(8,128)(2,1)S(1)} %copy.61) | copy-start | bytes 73732
  27.5 1.3 %copy-start.9 = (f32[128]{0:T(128)S(1)}, f32[128]{0:T(128)}, u32[]{:S(2)}) copy-start(f32[128]{0:T(128)} %param.20) | copy-start | bytes 1540
  29.6 62.3 %copy-start.4 = (bf16[8,12,128]{2,0,1:T(8,128)(2,1)}, bf16[8,12,128]{2,0,1:T(8,128)(2,1)S(1)}, u32[]{:S(2)}) copy-start(bf16[8,12,128]{2,0,1:T(8,128)(2,1)S(1)} %fusion.24) | copy-start | bytes 73732
  97.7 2.6 %copy-start.1 = (f32[16,12,512]{2,0,1:T(8,128)S(1)}, f32[16,12,512]{2,0,1:T(8,128)}, u32[]{:S(2)}) copy-start(f32[16,12,512]{2,0,1:T(8,128)} %get-tuple-element.34) | copy-start | bytes 1179652
  97.8 2.7 %copy-start.5 = (f32[16,12]{0,1:T(8,128)S(1)}, f32[16,12]{0,1:T(8,128)}, u32[]{:S(2)}) copy-start(f32[16,12]{0,1:T(8,128)} %get-tuple-element.33) | copy-start | bytes 2308
Sparse Core Ops, SparseCore 0:
  18.5 69.5 all-gather.1
where the time goes:
time: 109 us
  waiting for transfers between devices  57.3 us (53%)
  other arithmetic  16.6 us (15%)
  local copies, waits for them, and re-layouts  15.6 us (14%)
  between operations  15.1 us (14%)
  matrix products  3.94 us (4%)
    all_gather x1, waiting for transfers between devices, in_one_piece(): whole = lax.all_gather(both, axis, axis=dim, tiled=True)  57.3 us
    unnamed x26, local copies, waits for them, and re-layouts  5.92 us
    reduce_sum x4, other arithmetic, head_norm(): mean_square = jnp.mean(shaped * shaped, axis=-1, keepdims=True)  4 us
    split x1, local copies, waits for them, and re-layouts, in_one_piece(): jnp.split(whole, [sum(widths[:k]) for k in range(1, len(widths))], axis=a...  3.76 us
    mul x1, other arithmetic, rotate(): odd_part * sine_part  3.16 us
    dot_general x2, matrix products, partial_attend(): jnp.einsum('rhd,shd->rhs', query_heads, key_block.reshape(key_count, head...  2.82 us
  transfers between devices with their start and end apart: 1, of which 1 were waited for; matrix products, arithmetic and copies ran while one was open for 11% of the time, Pallas kernels for 0%

commit v1 on v0

v1 whole, which is shorter than its diff:
```python
import math

import jax
import jax.numpy as jnp
from jax import lax
from jax.experimental import pallas as pl
from jax.experimental.pallas import tpu as pltpu
from jax.sharding import PartitionSpec as P

HD = 128
GRID_W = 64
SIDE = 4
EPS = 1e-06
MASKED = -1e30
SCALE = HD ** (-0.5)

VM = pl.BlockSpec(memory_space=pltpu.VMEM)
SM = pl.BlockSpec(memory_space=pltpu.SMEM)


def split_index(i):
    return i // (SIDE * SIDE), (i // SIDE) % SIDE, i % SIDE


def join_index(x, z, y):
    return ((x % SIDE) * SIDE + z % SIDE) * SIDE + y % SIDE


def shift(value, dx=0, dz=0, dy=0):
    pairs = []
    for i in range(SIDE**3):
        x, z, y = split_index(i)
        pairs.append((i, join_index(x + dx, z + dz, y + dy)))
    return lax.ppermute(value, "seq", pairs)


def head_norm(x, gain):
    mean_square = jnp.mean(x * x, axis=-1, keepdims=True)
    return x * lax.rsqrt(mean_square + EPS) * gain


def prep_kernel(heads, half, place, order, q_ref, k_ref, v_ref, qg, kg, o0, o1, o2, o3, q_s, k_s):
    rows = q_ref.shape[0]
    lane = lax.broadcasted_iota(jnp.int32, (rows, HD), 1)
    row = lax.broadcasted_iota(jnp.int32, (rows, HD), 0)
    pair = lane // 2
    first = pair < 8
    second = pair < 36
    within = jnp.where(first, pair, jnp.where(second, pair - 8, pair - 36)).astype(jnp.float32)
    dim = jnp.where(first, 16.0, 56.0)
    frequency = jnp.exp(within / dim * (-2.0 * math.log(10000.0)))
    t = jnp.zeros((rows, HD), jnp.int32)
    u = t
    w = t
    for i in range(rows):
        p = order[i]
        inside = p % half
        t = jnp.where(row == i, p // half, t)
        u = jnp.where(row == i, inside // GRID_W, u)
        w = jnp.where(row == i, inside % GRID_W, w)
    coordinate = jnp.where(first, t, jnp.where(second, u, w)).astype(jnp.float32)
    angle = coordinate * frequency
    cosine = jnp.cos(angle)
    sine = jnp.sin(angle)
    even = lane % 2 == 0
    sine = jnp.where(even, -sine, sine)
    for src, gain, dst in ((q_ref, qg, q_s), (k_ref, kg, k_s)):
        g = gain[...]
        for h in range(heads):
            x = head_norm(src[:, h * HD : (h + 1) * HD].astype(jnp.float32), g)
            partner = jnp.where(even, pltpu.roll(x, HD - 1, 1), pltpu.roll(x, 1, 1))
            dst[:, h * HD : (h + 1) * HD] = (x * cosine + partner * sine).astype(jnp.bfloat16)
    width = heads // SIDE * HD
    y = place[2]
    for d, out in enumerate((o0, o1, o2, o3)):
        start = pl.multiple_of(((y + d) % SIDE) * width, HD)
        out[:, 0:width] = k_s[:, pl.ds(start, width)]
        out[:, width : 2 * width] = v_ref[:, pl.ds(start, width)]
        out[:, 2 * width : 3 * width] = q_s[:, pl.ds(start, width)]


def pack_kernel(a0, a1, a2, a3, kv, q):
    rows = a0.shape[0]
    width = q.shape[1]
    for j, a in enumerate((a0, a1, a2, a3)):
        kv[j * rows : (j + 1) * rows, :] = a[:, : 2 * width]
        q[j * rows : (j + 1) * rows, :] = a[:, 2 * width :]


def text_kernel(place, q_ref, k_ref, v_ref, qg, kg, q_out, k_out, v_out):
    for src, gain, dst in ((q_ref, qg, q_out), (k_ref, kg, k_out)):
        g = gain[...]
        for h in range(src.shape[1] // HD):
            cols = slice(h * HD, (h + 1) * HD)
            dst[:, cols] = head_norm(src[:, cols].astype(jnp.float32), g).astype(jnp.bfloat16)
    v_out[...] = v_ref[...]


def attend_kernel(place, length, kv0, kv1, kv2, kv3, q0, q1, q2, q3, qt, kt, vt, out):
    kvs, qs = (kv0, kv1, kv2, kv3), (q0, q1, q2, q3)
    width = qt.shape[1]
    heads = width // HD
    text_keys = kt.shape[0]
    image_rows = SIDE * q0.shape[0]
    rows = image_rows + qt.shape[0]
    keys = text_keys + SIDE * kv0.shape[0]
    z, y = place[1], place[2]
    column = lax.broadcasted_iota(jnp.int32, (rows, keys), 1)
    valid = (column >= text_keys) | (column + z * text_keys < length[0])
    lane = lax.broadcasted_iota(jnp.int32, (rows, HD), 1)
    stats = jnp.zeros((rows, HD), jnp.float32)
    blended = []
    for h in range(heads):
        cols = slice(h * HD, (h + 1) * HD)
        vcols = slice(width + h * HD, width + (h + 1) * HD)
        query = jnp.concatenate([r[:, cols] for r in qs] + [qt[:, cols]], axis=0)
        key = jnp.concatenate([kt[:, cols]] + [r[:, cols] for r in kvs], axis=0)
        value = jnp.concatenate([vt[:, cols]] + [r[:, vcols] for r in kvs], axis=0)
        s = lax.dot_general(query, key, (((1,), (1,)), ((), ())), preferred_element_type=jnp.float32)
        s = jnp.where(valid, s * SCALE, MASKED)
        m = jnp.max(s, axis=1, keepdims=True).astype(jnp.bfloat16).astype(jnp.float32)
        e = jnp.exp(s - m)
        l = jnp.sum(e, axis=1, keepdims=True)
        blended.append(jnp.dot(e.astype(jnp.bfloat16), value, preferred_element_type=jnp.float32))
        low = l - l.astype(jnp.bfloat16).astype(jnp.float32)
        stats = jnp.where(lane == h, m, stats)
        stats = jnp.where(lane == 8 + h, l, stats)
        stats = jnp.where(lane == 16 + h, low, stats)
    blended.append(stats)
    for dz in range(SIDE):
        for dy in range(SIDE):
            i = dz * SIDE + dy
            there = ((z + SIDE - dz) % SIDE) * SIDE + (y + SIDE - dy) % SIDE
            for c, part in enumerate(blended):
                cols = slice(c * HD, (c + 1) * HD)
                out[there, 0:8, cols] = part[i * 8 : (i + 1) * 8].astype(jnp.bfloat16)
                begin = image_rows + i * 8
                out[i, 8:16, cols] = part[begin : begin + 8].astype(jnp.bfloat16)


def combine_kernel(got, image_out, text_out):
    heads = (got.shape[2] - HD) // HD
    width = heads * HD
    half = image_out.shape[0]
    for y in range(SIDE):
        stats = [got[z * SIDE + y, :, width:].astype(jnp.float32) for z in range(SIDE)]
        top = stats[0]
        for s in stats[1:]:
            top = jnp.maximum(top, s)
        factors = [jnp.exp(s - top) for s in stats]
        total = 0.0
        for s, f in zip(stats, factors):
            total = total + f * (pltpu.roll(s, HD - 8, 1) + pltpu.roll(s, HD - 16, 1))
        for h in range(heads):
            inverse = 1.0 / total[:, h : h + 1]
            acc = 0.0
            for z in range(SIDE):
                part = got[z * SIDE + y, :, h * HD : (h + 1) * HD].astype(jnp.float32)
                acc = acc + part * (factors[z][:, h : h + 1] * inverse)
            cols = slice(y * width + h * HD, y * width + (h + 1) * HD)
            image_out[:, cols] = acc[:half].astype(jnp.bfloat16)
            text_out[:, cols] = acc[half:].astype(jnp.bfloat16)


def local(
    image_query,
    image_key,
    image_value,
    text_query,
    text_key,
    text_value,
    image_query_gain,
    image_key_gain,
    text_query_gain,
    text_key_gain,
    image_order,
    text_length,
):
    rows, model = image_query.shape
    heads = model // HD
    width = model // SIDE
    text_rows = text_query.shape[0]
    block = text_rows // SIDE
    half = rows * SIDE**3 // 2
    x, z, y = split_index(lax.axis_index("seq"))
    place = jnp.stack([x, z, y]).astype(jnp.int32)
    bf = jnp.bfloat16
    struct = jax.ShapeDtypeStruct
    gains = [g.reshape(1, HD) for g in (image_query_gain, image_key_gain, text_query_gain, text_key_gain)]

    own = pl.pallas_call(
        lambda *refs: prep_kernel(heads, half, *refs),
        out_shape=[struct((rows, 3 * width), bf)] * SIDE,
        in_specs=[SM, SM] + [VM] * 5,
        out_specs=[VM] * SIDE,
        scratch_shapes=[pltpu.VMEM((rows, model), bf)] * 2,
        name="prep",
    )(place, image_order, image_query, image_key, image_value, gains[0], gains[1])

    from_y = [own[0]] + [shift(own[d], dy=d) for d in range(1, SIDE)]

    qt, kt, vt = pl.pallas_call(
        text_kernel,
        out_shape=[struct((block, width), bf)] * 3,
        grid_spec=pltpu.PrefetchScalarGridSpec(
            num_scalar_prefetch=1,
            grid=(1,),
            in_specs=[
                pl.BlockSpec((block, width), lambda i, p: (p[0], p[2])),
                pl.BlockSpec((block, width), lambda i, p: (p[1], p[2])),
                pl.BlockSpec((block, width), lambda i, p: (p[1], p[2])),
                pl.BlockSpec((1, HD), lambda i, p: (0, 0)),
                pl.BlockSpec((1, HD), lambda i, p: (0, 0)),
            ],
            out_specs=[pl.BlockSpec((block, width), lambda i, p: (0, 0))] * 3,
        ),
        cost_estimate=pl.CostEstimate(flops=20_000_000, bytes_accessed=600_000, transcendentals=0),
        name="text",
    )(place, text_query, text_key, text_value, gains[2], gains[3])

    kv, q = pl.pallas_call(
        pack_kernel,
        out_shape=[struct((SIDE * rows, 2 * width), bf), struct((SIDE * rows, width), bf)],
        in_specs=[VM] * SIDE,
        out_specs=[VM] * 2,
        name="pack",
    )(*from_y)

    kvs = [kv] + [shift(kv, dx=d) for d in range(1, SIDE)]
    qs = [q] + [shift(q, dz=d) for d in range(1, SIDE)]

    parts = SIDE * SIDE
    out_rows = rows + text_rows // SIDE**3
    partial = pl.pallas_call(
        attend_kernel,
        out_shape=struct((parts, out_rows, width + HD), bf),
        in_specs=[SM, SM] + [VM] * 11,
        out_specs=VM,
        name="attend",
    )(place, text_length, *kvs, *qs, qt, kt, vt)

    groups = [[x * parts + i for i in range(parts)] for x in range(SIDE)]
    got = lax.all_to_all(partial, "seq", 0, 0, axis_index_groups=groups, tiled=True)

    return pl.pallas_call(
        combine_kernel,
        out_shape=[struct((rows, model), bf), struct((out_rows - rows, model), bf)],
        in_specs=[VM],
        out_specs=[VM] * 2,
        name="combine",
    )(got)


def solution(mesh):
    token = P(("req", "seq"), None)
    text = P("req", None)
    return jax.shard_map(
        lambda *args: tuple(local(*args)),
        mesh=mesh,
        in_specs=(token, token, token, text, text, text, P(), P(), P(), P(), P(("req", "seq")), P("req")),
        out_specs=(token, token),
        check_vma=False,
    )
```

time: 109 us -> 49 us (0.45)
  waiting for transfers between devices: 57.3 us -> 3.76 us
  other arithmetic: 16.6 us -> 0.61 us
  starting transfers between devices: 0.04 us -> 15.7 us
  local copies, waits for them, and re-layouts: 15.6 us -> 1.22 us
  blocking collectives: 0 us -> 14.1 us
  between operations: 15.1 us -> 1.39 us
  Pallas kernels: 0 us -> 11.5 us
  matrix products: 3.94 us -> 0 us
    all_gather x1 -> x0, waiting for transfers between devices: 57.3 us -> none  [in_one_piece(): whole = lax.all_gather(both, axis, axis=dim, tiled=True)]
    ppermute x0 -> x9, starting transfers between devices: none -> 15.7 us  [shift(): return lax.ppermute(value, 'seq', pairs)]
    all_to_all x0 -> x1, blocking collectives: none -> 14.1 us  [local(): lax.all_to_all(partial, 'seq', 0, 0, axis_index_groups=groups, tiled=True)]
    pallas_call x0 -> x5, Pallas kernels: none -> 11.5 us  [the longest x1 2.97 us: local(): pl.pallas_call(lambda *refs: prep_kernel(heads, half, *refs), out_shape=[...]
    mul x3 -> x0, other arithmetic: 6.2 us -> none  [the longest x1 3.16 us: rotate(): odd_part * sine_part]
    reduce_sum x6 -> x0, other arithmetic: 6.08 us -> none  [the longest x4 4 us: head_norm(): mean_square = jnp.mean(shaped * shaped, axis=-1, keepdims=True)]
    unnamed x26 -> x18, local copies, waits for them, and re-layouts: 5.92 us -> 1.22 us
    dot_general x4 -> x0, matrix products: 3.94 us -> none  [the longest x2 2.82 us: partial_attend(): jnp.einsum('rhd,shd->rhs', query_heads, key_block.reshape(key_count, head...]
  transfers between devices with their start and end apart: 1 -> 9, of which waited for: 1 -> 3; matrix products, arithmetic and copies ran while one was open for 11% -> 0% of each run, Pallas kernels for 0% -> 5%
where the time goes in v1:
time: 49 us; the launch traced here: 48.3 us
  starting transfers between devices  15.7 us (32%)
  blocking collectives  14.1 us (29%)
  Pallas kernels  11.5 us (23%)
  waiting for transfers between devices  3.76 us (8%)
  between operations  1.39 us (3%)
  local copies, waits for them, and re-layouts  1.22 us (2%)
  other arithmetic  0.61 us (1%)
    ppermute x9, starting transfers between devices, shift(): return lax.ppermute(value, 'seq', pairs)  15.7 us
    all_to_all x1, blocking collectives, local(): lax.all_to_all(partial, 'seq', 0, 0, axis_index_groups=groups, tiled=True)  14.1 us
    ppermute x9, waiting for transfers between devices, shift(): return lax.ppermute(value, 'seq', pairs)  3.76 us
    pallas_call x1, Pallas kernels, local(): pl.pallas_call(lambda *refs: prep_kernel(heads, half, *refs), out_shape=[...  2.97 us
    pallas_call x1, Pallas kernels, local(): pl.pallas_call(attend_kernel, out_shape=struct((parts, out_rows, width +...  2.67 us
    pallas_call x1, Pallas kernels, local(): pl.pallas_call(text_kernel, out_shape=[struct((block, width), bf)] * 3, g...  2.54 us
    pallas_call x1, Pallas kernels, local(): pl.pallas_call(combine_kernel, out_shape=[struct((rows, model), bf), stru...  1.93 us
    pallas_call x1, Pallas kernels, local(): pl.pallas_call(pack_kernel, out_shape=[struct((SIDE * rows, 2 * width), b...  1.4 us
  transfers between devices with their start and end apart: 9, of which 3 were waited for; matrix products, arithmetic and copies ran while one was open for 0% of the time, Pallas kernels for 5%

profile of v1, /device:TPU:0, one launch (start us, length us, event | category | flops | bytes accessed | tf_op | source)
XLA Modules:
  0.0 48.3 jit_solution(11614767774900638345)
XLA Ops:
  0.7 0.6 %pad_add_fusion.refs_0_.place = s32[3]{0:T(128)} fusion(s32[1]{0:T(128)} %bitcast.2, s32[1]{0:T(128)} %bitcast.1, s32[1]{0:T(128)} %bitcast), kind=kLoop, calls=%fused_computation | loop fusion | flops 6 | bytes 24 | tf_op jit(solution)/shard_map/stack | solution.py:186
  1.3 3.0 %prep.1 = (bf16[8,1152]{1,0:T(8,128)(2,1)}, bf16[8,1152]{1,0:T(8,128)(2,1)}, bf16[8,1152]{1,0:T(8,128)(2,1)}, bf16[8,1152]{1,0:T(8,128)(2,1)}) custom-call(s32[3]{0:T(128)} %pad_add_fusion.refs_0_.place, s32[8]{0:T(128)} %refs_1_.1, bf16[8,1536]{1,0:T(8,128)(2,1)} %refs_2_.1, bf16[8,1536]{1,0:T(8,128)(2,1)} %refs_3_.1, bf16[8,1536]{1,0:T(8,128)(2,1)} %refs_4_.1, ...), custom_call_target="tpu_custom_call" | custom-call | tf_op jit(solution)/shard_map/prep/pallas_call | solution.py:191
  4.3 1.7 %collective-permute-start = (bf16[8,1152]{1,0:T(8,128)(2,1)}, bf16[8,1152]{1,0:T(8,128)(2,1)S(1)}, u32[]{:S(2)}, u32[]{:S(2)}) collective-permute-start(bf16[8,1152]{1,0:T(8,128)(2,1)} %get-tuple-element.12), channel_id=1, source_target_pairs={{0,1},{1,2},{2,3},{3,0},{4,5},{5,6},{6,7},{7,4},{8,9},{9,10},{10,1... | collective-permute-start | bytes 55304 | tf_op jit(solution)/shard_map/ppermute | solution.py:34
  5.9 2.9 %collective-permute-start.1 = (bf16[8,1152]{1,0:T(8,128)(2,1)}, bf16[8,1152]{1,0:T(8,128)(2,1)S(1)}, u32[]{:S(2)}, u32[]{:S(2)}) collective-permute-start(bf16[8,1152]{1,0:T(8,128)(2,1)} %get-tuple-element.13), channel_id=1, source_target_pairs={{0,2},{1,3},{2,0},{3,1},{4,6},{5,7},{6,4},{7,5},{8,10},{9,11},{10,... | collective-permute-start | bytes 55304 | tf_op jit(solution)/shard_map/ppermute | solution.py:34
  8.9 1.3 %collective-permute-start.2 = (bf16[8,1152]{1,0:T(8,128)(2,1)}, bf16[8,1152]{1,0:T(8,128)(2,1)S(1)}, u32[]{:S(2)}, u32[]{:S(2)}) collective-permute-start(bf16[8,1152]{1,0:T(8,128)(2,1)} %get-tuple-element.14), channel_id=1, source_target_pairs={{0,3},{1,0},{2,1},{3,2},{4,7},{5,4},{6,5},{7,6},{8,11},{9,8},{10,9... | collective-permute-start | bytes 55304 | tf_op jit(solution)/shard_map/ppermute | solution.py:34
  10.2 0.0 collective-permute-done.a1
  10.2 1.2 %collective-permute-done.1.a2 = bf16[8,1152]{1,0:T(8,128)(2,1)S(1)} collective-permute-done((bf16[8,1152]{1,0:T(8,128)(2,1)}, bf16[8,1152]{1,0:T(8,128)(2,1)S(1)}, u32[]{:S(2)}, u32[]{:S(2)}) %collective-permute-start.1) | collective-permute-done | bytes 18464 | tf_op jit(solution)/shard_map/ppermute | solution.py:34
  11.4 1.4 %collective-permute-done.2.a3 = bf16[8,1152]{1,0:T(8,128)(2,1)S(1)} collective-permute-done((bf16[8,1152]{1,0:T(8,128)(2,1)}, bf16[8,1152]{1,0:T(8,128)(2,1)S(1)}, u32[]{:S(2)}, u32[]{:S(2)}) %collective-permute-start.2) | collective-permute-done | bytes 18464 | tf_op jit(solution)/shard_map/ppermute | solution.py:34
  12.8 0.6 %copy-done.8 = bf16[8,1152]{1,0:T(8,128)(2,1)} copy-done((bf16[8,1152]{1,0:T(8,128)(2,1)}, bf16[8,1152]{1,0:T(8,128)(2,1)S(1)}, u32[]{:S(2)}) %copy-start.8) | copy-done | bytes 18456
  13.4 1.4 %pack.1 = (bf16[32,768]{1,0:T(8,128)(2,1)}, bf16[32,384]{1,0:T(8,128)(2,1)}) custom-call(bf16[8,1152]{1,0:T(8,128)(2,1)} %get-tuple-element.11.a0, bf16[8,1152]{1,0:T(8,128)(2,1)} %copy-done.6, bf16[8,1152]{1,0:T(8,128)(2,1)} %copy-done.7, bf16[8,1152]{1,0:T(8,128)(2,1)} %copy-done.8), custom_call_target="tpu_custom_call" | custom-call | tf_op jit(solution)/shard_map/pack/pallas_call | solution.py:221
  14.8 4.0 %collective-permute-start.8 = (bf16[32,384]{1,0:T(8,128)(2,1)}, bf16[32,384]{1,0:T(8,128)(2,1)S(1)}, u32[]{:S(2)}, u32[]{:S(2)}) collective-permute-start(bf16[32,384]{1,0:T(8,128)(2,1)} %get-tuple-element.16.q0), channel_id=1, source_target_pairs={{0,12},{1,13},{2,14},{3,15},{4,0},{5,1},{6,2},{7,3},{8,4},{9,5},{1... | collective-permute-start | bytes 73736 | tf_op jit(solution)/shard_map/ppermute | solution.py:34
  18.9 2.8 %collective-permute-start.5 = (bf16[32,768]{1,0:T(8,128)(2,1)}, bf16[32,768]{1,0:T(8,128)(2,1)S(1)}, u32[]{:S(2)}, u32[]{:S(2)}) collective-permute-start(bf16[32,768]{1,0:T(8,128)(2,1)} %get-tuple-element.15.kv0), channel_id=1, source_target_pairs={{0,48},{1,49},{2,50},{3,51},{4,52},{5,53},{6,54},{7,55},{8,56},{9,... | collective-permute-start | bytes 147464 | tf_op jit(solution)/shard_map/ppermute | solution.py:34
  21.6 0.8 %collective-permute-start.4 = (bf16[32,768]{1,0:T(8,128)(2,1)}, bf16[32,768]{1,0:T(8,128)(2,1)S(1)}, u32[]{:S(2)}, u32[]{:S(2)}) collective-permute-start(bf16[32,768]{1,0:T(8,128)(2,1)} %get-tuple-element.15.kv0), channel_id=1, source_target_pairs={{0,32},{1,33},{2,34},{3,35},{4,36},{5,37},{6,38},{7,39},{8,40},{9,... | collective-permute-start | bytes 147464 | tf_op jit(solution)/shard_map/ppermute | solution.py:34
  22.4 0.9 %collective-permute-start.3 = (bf16[32,768]{1,0:T(8,128)(2,1)}, bf16[32,768]{1,0:T(8,128)(2,1)S(1)}, u32[]{:S(2)}, u32[]{:S(2)}) collective-permute-start(bf16[32,768]{1,0:T(8,128)(2,1)} %get-tuple-element.15.kv0), channel_id=1, source_target_pairs={{0,16},{1,17},{2,18},{3,19},{4,20},{5,21},{6,22},{7,23},{8,24},{9,... | collective-permute-start | bytes 147464 | tf_op jit(solution)/shard_map/ppermute | solution.py:34
  23.3 0.0 collective-permute-start.7
  23.3 1.3 %collective-permute-start.6 = (bf16[32,384]{1,0:T(8,128)(2,1)}, bf16[32,384]{1,0:T(8,128)(2,1)S(1)}, u32[]{:S(2)}, u32[]{:S(2)}) collective-permute-start(bf16[32,384]{1,0:T(8,128)(2,1)} %get-tuple-element.16.q0), channel_id=1, source_target_pairs={{0,4},{1,5},{2,6},{3,7},{4,8},{5,9},{6,10},{7,11},{8,12},{9,13},{1... | collective-permute-start | bytes 73736 | tf_op jit(solution)/shard_map/ppermute | solution.py:34
  25.2 2.5 %text.1 = (bf16[128,384]{1,0:T(8,128)(2,1)}, bf16[128,384]{1,0:T(8,128)(2,1)}, bf16[128,384]{1,0:T(8,128)(2,1)}) custom-call(s32[3]{0:T(128)} %pad_add_fusion.refs_0_.place, bf16[512,1536]{1,0:T(8,128)(2,1)} %q_ref.1, bf16[512,1536]{1,0:T(8,128)(2,1)} %k_ref.1, bf16[512,1536]{1,0:T(8,128)(2,1)} %v_ref.1, f32[1,128]{1,0:T(1,128)} %bitcast.9, f32[1,128]{1,0:T(1,128)} %bitcast.10), custom_call_target="tpu_custom_call" | custom-call | flops 20000000 | bytes 600000 | tf_op jit(solution)/shard_map/text/pallas_call | solution.py:202
  27.8 1.1 %collective-permute-done.7.q2 = bf16[32,384]{1,0:T(8,128)(2,1)S(1)} collective-permute-done((bf16[32,384]{1,0:T(8,128)(2,1)}, bf16[32,384]{1,0:T(8,128)(2,1)S(1)}, u32[]{:S(2)}, u32[]{:S(2)}) %collective-permute-start.7) | collective-permute-done | bytes 24608 | tf_op jit(solution)/shard_map/ppermute | solution.py:34
  29.0 0.6 %copy-done.4 = bf16[32,384]{1,0:T(8,128)(2,1)} copy-done((bf16[32,384]{1,0:T(8,128)(2,1)}, bf16[32,384]{1,0:T(8,128)(2,1)S(1)}, u32[]{:S(2)}) %copy-start.4) | copy-done | bytes 24600
  29.5 0.0 copy-done
  29.5 0.0 copy-done.1
  29.6 2.7 %attend.1 = bf16[16,16,512]{2,1,0:T(8,128)(2,1)} custom-call(s32[3]{0:T(128)} %pad_add_fusion.refs_0_.place, s32[1]{0:T(128)S(6)} %copy.14.length, bf16[32,768]{1,0:T(8,128)(2,1)} %get-tuple-element.15.kv0, bf16[32,768]{1,0:T(8,128)(2,1)} %copy-done.2, bf16[32,768]{1,0:T(8,128)(2,1)} %copy-done.1, bf16[32,768]{1,0:T(8,128)(2,1)} %copy-done, ...), custom_call_target="tpu_custom_call" | custom-call | tf_op jit(solution)/shard_map/attend/pallas_call | solution.py:234
  32.3 14.1 %all_to_all.5.got = bf16[16,16,512]{2,1,0:T(8,128)(2,1)} all-to-all(bf16[16,16,512]{2,1,0:T(8,128)(2,1)} %attend.1), channel_id=1, replica_groups={{0,1,2,3,4,5,6,7,8,9,10,11,12,13,14,15},{16,17,18,19,20,21,22,23,24,25,..., dimensions={0} | all-to-all | bytes 524288 | tf_op jit(solution)/shard_map/all_to_all | solution.py:243
  46.4 1.9 %combine.1 = (bf16[8,1536]{1,0:T(8,128)(2,1)}, bf16[8,1536]{1,0:T(8,128)(2,1)}) custom-call(bf16[16,16,512]{2,1,0:T(8,128)(2,1)} %all_to_all.5.got), custom_call_target="tpu_custom_call" | custom-call | tf_op jit(solution)/shard_map/combine/pallas_call | solution.py:245
  (19 shorter events, 0.0 us)
Async XLA Ops:
  4.3 5.9 %collective-permute-start = (bf16[8,1152]{1,0:T(8,128)(2,1)}, bf16[8,1152]{1,0:T(8,128)(2,1)S(1)}, u32[]{:S(2)}, u32[]{:S(2)}) collective-permute-start(bf16[8,1152]{1,0:T(8,128)(2,1)} %get-tuple-element.12), channel_id=1, source_target_pairs={{0,1},{1,2},{2,3},{3,0},{4,5},{5,6},{6,7},{7,4},{8,9},{9,10},{10,1... | collective-permute-start | bytes 55304 | tf_op jit(solution)/shard_map/ppermute | solution.py:34
  5.9 5.5 %collective-permute-start.1 = (bf16[8,1152]{1,0:T(8,128)(2,1)}, bf16[8,1152]{1,0:T(8,128)(2,1)S(1)}, u32[]{:S(2)}, u32[]{:S(2)}) collective-permute-start(bf16[8,1152]{1,0:T(8,128)(2,1)} %get-tuple-element.13), channel_id=1, source_target_pairs={{0,2},{1,3},{2,0},{3,1},{4,6},{5,7},{6,4},{7,5},{8,10},{9,11},{10,... | collective-permute-start | bytes 55304 | tf_op jit(solution)/shard_map/ppermute | solution.py:34
  8.9 4.0 %collective-permute-start.2 = (bf16[8,1152]{1,0:T(8,128)(2,1)}, bf16[8,1152]{1,0:T(8,128)(2,1)S(1)}, u32[]{:S(2)}, u32[]{:S(2)}) collective-permute-start(bf16[8,1152]{1,0:T(8,128)(2,1)} %get-tuple-element.14), channel_id=1, source_target_pairs={{0,3},{1,0},{2,1},{3,2},{4,7},{5,4},{6,5},{7,6},{8,11},{9,8},{10,9... | collective-permute-start | bytes 55304 | tf_op jit(solution)/shard_map/ppermute | solution.py:34
  10.2 2.6 %copy-start.6 = (bf16[8,1152]{1,0:T(8,128)(2,1)}, bf16[8,1152]{1,0:T(8,128)(2,1)S(1)}, u32[]{:S(2)}) copy-start(bf16[8,1152]{1,0:T(8,128)(2,1)S(1)} %collective-permute-done.a1) | copy-start | bytes 55300
  11.4 1.4 %copy-start.7 = (bf16[8,1152]{1,0:T(8,128)(2,1)}, bf16[8,1152]{1,0:T(8,128)(2,1)S(1)}, u32[]{:S(2)}) copy-start(bf16[8,1152]{1,0:T(8,128)(2,1)S(1)} %collective-permute-done.1.a2) | copy-start | bytes 55300
  12.8 0.6 %copy-start.8 = (bf16[8,1152]{1,0:T(8,128)(2,1)}, bf16[8,1152]{1,0:T(8,128)(2,1)S(1)}, u32[]{:S(2)}) copy-start(bf16[8,1152]{1,0:T(8,128)(2,1)S(1)} %collective-permute-done.2.a3) | copy-start | bytes 55300
  14.8 8.5 %collective-permute-start.8 = (bf16[32,384]{1,0:T(8,128)(2,1)}, bf16[32,384]{1,0:T(8,128)(2,1)S(1)}, u32[]{:S(2)}, u32[]{:S(2)}) collective-permute-start(bf16[32,384]{1,0:T(8,128)(2,1)} %get-tuple-element.16.q0), channel_id=1, source_target_pairs={{0,12},{1,13},{2,14},{3,15},{4,0},{5,1},{6,2},{7,3},{8,4},{9,5},{1... | collective-permute-start | bytes 73736 | tf_op jit(solution)/shard_map/ppermute | solution.py:34
  18.9 10.0 %collective-permute-start.5 = (bf16[32,768]{1,0:T(8,128)(2,1)}, bf16[32,768]{1,0:T(8,128)(2,1)S(1)}, u32[]{:S(2)}, u32[]{:S(2)}) collective-permute-start(bf16[32,768]{1,0:T(8,128)(2,1)} %get-tuple-element.15.kv0), channel_id=1, source_target_pairs={{0,48},{1,49},{2,50},{3,51},{4,52},{5,53},{6,54},{7,55},{8,56},{9,... | collective-permute-start | bytes 147464 | tf_op jit(solution)/shard_map/ppermute | solution.py:34
  21.6 7.3 %collective-permute-start.4 = (bf16[32,768]{1,0:T(8,128)(2,1)}, bf16[32,768]{1,0:T(8,128)(2,1)S(1)}, u32[]{:S(2)}, u32[]{:S(2)}) collective-permute-start(bf16[32,768]{1,0:T(8,128)(2,1)} %get-tuple-element.15.kv0), channel_id=1, source_target_pairs={{0,32},{1,33},{2,34},{3,35},{4,36},{5,37},{6,38},{7,39},{8,40},{9,... | collective-permute-start | bytes 147464 | tf_op jit(solution)/shard_map/ppermute | solution.py:34
  22.4 6.5 %collective-permute-start.3 = (bf16[32,768]{1,0:T(8,128)(2,1)}, bf16[32,768]{1,0:T(8,128)(2,1)S(1)}, u32[]{:S(2)}, u32[]{:S(2)}) collective-permute-start(bf16[32,768]{1,0:T(8,128)(2,1)} %get-tuple-element.15.kv0), channel_id=1, source_target_pairs={{0,16},{1,17},{2,18},{3,19},{4,20},{5,21},{6,22},{7,23},{8,24},{9,... | collective-permute-start | bytes 147464 | tf_op jit(solution)/shard_map/ppermute | solution.py:34
  23.3 5.6 %collective-permute-start.7 = (bf16[32,384]{1,0:T(8,128)(2,1)}, bf16[32,384]{1,0:T(8,128)(2,1)S(1)}, u32[]{:S(2)}, u32[]{:S(2)}) collective-permute-start(bf16[32,384]{1,0:T(8,128)(2,1)} %get-tuple-element.16.q0), channel_id=1, source_target_pairs={{0,8},{1,9},{2,10},{3,11},{4,12},{5,13},{6,14},{7,15},{8,0},{9,1},... | collective-permute-start | bytes 73736 | tf_op jit(solution)/shard_map/ppermute | solution.py:34
  23.3 4.5 %copy-start.3 = (bf16[32,384]{1,0:T(8,128)(2,1)}, bf16[32,384]{1,0:T(8,128)(2,1)S(1)}, u32[]{:S(2)}) copy-start(bf16[32,384]{1,0:T(8,128)(2,1)S(1)} %collective-permute-done.8.q3) | copy-start | bytes 73732
  23.3 5.6 %collective-permute-start.6 = (bf16[32,384]{1,0:T(8,128)(2,1)}, bf16[32,384]{1,0:T(8,128)(2,1)S(1)}, u32[]{:S(2)}, u32[]{:S(2)}) collective-permute-start(bf16[32,384]{1,0:T(8,128)(2,1)} %get-tuple-element.16.q0), channel_id=1, source_target_pairs={{0,4},{1,5},{2,6},{3,7},{4,8},{5,9},{6,10},{7,11},{8,12},{9,13},{1... | collective-permute-start | bytes 73736 | tf_op jit(solution)/shard_map/ppermute | solution.py:34
  28.9 0.6 %copy-start.4 = (bf16[32,384]{1,0:T(8,128)(2,1)}, bf16[32,384]{1,0:T(8,128)(2,1)S(1)}, u32[]{:S(2)}) copy-start(bf16[32,384]{1,0:T(8,128)(2,1)S(1)} %collective-permute-done.7.q2) | copy-start | bytes 73732
  28.9 0.6 %copy-start.5 = (bf16[32,384]{1,0:T(8,128)(2,1)}, bf16[32,384]{1,0:T(8,128)(2,1)S(1)}, u32[]{:S(2)}) copy-start(bf16[32,384]{1,0:T(8,128)(2,1)S(1)} %collective-permute-done.6.q1) | copy-start | bytes 73732
  28.9 0.6 %copy-start = (bf16[32,768]{1,0:T(8,128)(2,1)}, bf16[32,768]{1,0:T(8,128)(2,1)S(1)}, u32[]{:S(2)}) copy-start(bf16[32,768]{1,0:T(8,128)(2,1)S(1)} %collective-permute-done.5.kv3) | copy-start | bytes 147460
  28.9 0.6 %copy-start.1 = (bf16[32,768]{1,0:T(8,128)(2,1)}, bf16[32,768]{1,0:T(8,128)(2,1)S(1)}, u32[]{:S(2)}) copy-start(bf16[32,768]{1,0:T(8,128)(2,1)S(1)} %collective-permute-done.4.kv2) | copy-start | bytes 147460
  29.0 0.6 %copy-start.2 = (bf16[32,768]{1,0:T(8,128)(2,1)}, bf16[32,768]{1,0:T(8,128)(2,1)S(1)}, u32[]{:S(2)}) copy-start(bf16[32,768]{1,0:T(8,128)(2,1)S(1)} %collective-permute-done.3.kv1) | copy-start | bytes 147460

commit v2 on v1

v2 whole, which is shorter than its diff:
```python
import jax
import jax.numpy as jnp
import numpy as np
from jax import lax
from jax.experimental import pallas as pl
from jax.experimental.pallas import tpu as pltpu
from jax.sharding import PartitionSpec as P

HD = 128
GRID_W = 64
SIDE = 4
EPS = 1e-06
MASKED = -1e30
SCALE = HD ** (-0.5)

VM = pl.BlockSpec(memory_space=pltpu.VMEM)
SM = pl.BlockSpec(memory_space=pltpu.SMEM)
ANY = pl.BlockSpec(memory_space=pl.ANY)


def split_index(i):
    return i // (SIDE * SIDE), (i // SIDE) % SIDE, i % SIDE


def join_index(x, z, y):
    return ((x % SIDE) * SIDE + z % SIDE) * SIDE + y % SIDE


def shift(value, dx=0, dz=0, dy=0):
    pairs = []
    for i in range(SIDE**3):
        x, z, y = split_index(i)
        pairs.append((i, join_index(x + dx, z + dz, y + dy)))
    return in_vmem(lax.ppermute(value, "seq", pairs))


def in_vmem(value):
    return pltpu.with_memory_space_constraint(value, pltpu.VMEM)


def head_norm(x, gain):
    mean_square = jnp.mean(x * x, axis=-1, keepdims=True)
    return x * lax.rsqrt(mean_square + EPS) * gain


def frequencies():
    pair = np.arange(HD) // 2
    within = np.where(pair < 8, pair, np.where(pair < 36, pair - 8, pair - 36)).astype(np.float64)
    dim = np.where(pair < 8, 16.0, 56.0)
    return (10000.0 ** (-2.0 * within / dim)).astype(np.float32).reshape(1, HD)


def load(pairs, sems):
    copies = [pltpu.make_async_copy(src, dst, sems.at[i]) for i, (src, dst) in enumerate(pairs)]
    for c in copies:
        c.start()
    for c in copies:
        c.wait()


def prep_kernel(heads, half, order_h, freq_h, q_h, k_h, v_h, qg_h, kg_h, o0, o1, o2, o3, order, freq, q_in, k_in, v_in, qg, kg, q_s, k_s, sems):
    load(
        ((order_h, order), (freq_h, freq), (q_h, q_in), (k_h, k_in), (v_h, v_in), (qg_h, qg), (kg_h, kg)),
        sems,
    )
    rows = q_in.shape[0]
    lane = lax.broadcasted_iota(jnp.int32, (rows, HD), 1)
    row = lax.broadcasted_iota(jnp.int32, (rows, HD), 0)
    pair = lane // 2
    t = jnp.zeros((rows, HD), jnp.int32)
    u = t
    w = t
    for i in range(rows):
        p = order[i]
        inside = p % half
        t = jnp.where(row == i, p // half, t)
        u = jnp.where(row == i, inside // GRID_W, u)
        w = jnp.where(row == i, inside % GRID_W, w)
    coordinate = jnp.where(pair < 8, t, jnp.where(pair < 36, u, w)).astype(jnp.float32)
    angle = coordinate * freq[...]
    cosine = jnp.cos(angle)
    sine = jnp.sin(angle)
    even = lane % 2 == 0
    sine = jnp.where(even, -sine, sine)
    for src, gain, dst in ((q_in, qg, q_s), (k_in, kg, k_s)):
        g = gain[...]
        for h in range(heads):
            x = head_norm(src[:, h * HD : (h + 1) * HD].astype(jnp.float32), g)
            partner = jnp.where(even, pltpu.roll(x, HD - 1, 1), pltpu.roll(x, 1, 1))
            dst[:, h * HD : (h + 1) * HD] = (x * cosine + partner * sine).astype(jnp.bfloat16)
    width = heads // SIDE * HD
    y = lax.axis_index("seq") % SIDE
    for d, out in enumerate((o0, o1, o2, o3)):
        start = pl.multiple_of(((y + d) % SIDE) * width, HD)
        out[:, 0:width] = k_s[:, pl.ds(start, width)]
        out[:, width : 2 * width] = v_in[:, pl.ds(start, width)]
        out[:, 2 * width : 3 * width] = q_s[:, pl.ds(start, width)]


def pack_kernel(a0, a1, a2, a3, order_only, kv, q):
    rows = a0.shape[0]
    width = q.shape[1]
    for j, a in enumerate((a0, a1, a2, a3)):
        kv[j * rows : (j + 1) * rows, :] = a[:, : 2 * width]
        q[j * rows : (j + 1) * rows, :] = a[:, 2 * width :]


def text_kernel(q_h, k_h, v_h, qg_h, kg_h, length_h, q_out, k_out, v_out, bias, length, q_in, k_in, qg, kg, sems):
    block, width = q_in.shape
    x, z, y = split_index(lax.axis_index("seq"))
    cols = pl.ds(pl.multiple_of(y * width, HD), width)
    q_rows = pl.ds(pl.multiple_of(x * block, block), block)
    k_rows = pl.ds(pl.multiple_of(z * block, block), block)
    load(
        (
            (length_h, length),
            (q_h.at[q_rows, cols], q_in),
            (k_h.at[k_rows, cols], k_in),
            (v_h.at[k_rows, cols], v_out),
            (qg_h, qg),
            (kg_h, kg),
        ),
        sems,
    )
    for src, gain, dst in ((q_in, qg, q_out), (k_in, kg, k_out)):
        g = gain[...]
        for h in range(width // HD):
            at = slice(h * HD, (h + 1) * HD)
            dst[:, at] = head_norm(src[:, at].astype(jnp.float32), g).astype(jnp.bfloat16)
    key = lax.broadcasted_iota(jnp.int32, bias.shape, 1) + z * block
    bias[...] = jnp.where(key < length[0], 0.0, MASKED)


def attend_kernel(kv0, kv1, kv2, kv3, q0, q1, q2, q3, qt, kt, vt, bias, out):
    kvs, qs = (kv0, kv1, kv2, kv3), (q0, q1, q2, q3)
    width = qt.shape[1]
    heads = width // HD
    text_keys = kt.shape[0]
    image_rows = SIDE * q0.shape[0]
    rows = image_rows + qt.shape[0]
    _, z, y = split_index(lax.axis_index("seq"))
    masked = bias[0:1, :]
    lane = lax.broadcasted_iota(jnp.int32, (rows, HD), 1)
    stats = jnp.zeros((rows, HD), jnp.float32)
    blended = []
    for h in range(heads):
        cols = slice(h * HD, (h + 1) * HD)
        vcols = slice(width + h * HD, width + (h + 1) * HD)
        query = jnp.concatenate([r[:, cols] for r in qs] + [qt[:, cols]], axis=0)
        key = jnp.concatenate([kt[:, cols]] + [r[:, cols] for r in kvs], axis=0)
        value = jnp.concatenate([vt[:, cols]] + [r[:, vcols] for r in kvs], axis=0)
        s = lax.dot_general(query, key, (((1,), (1,)), ((), ())), preferred_element_type=jnp.float32)
        s = jnp.concatenate([s[:, :text_keys] * SCALE + masked, s[:, text_keys:] * SCALE], axis=1)
        m = jnp.max(s, axis=1, keepdims=True)
        e = jnp.exp(s - m)
        l = jnp.sum(e, axis=1, keepdims=True)
        blended.append(jnp.dot(e.astype(jnp.bfloat16), value, preferred_element_type=jnp.float32))
        for first, value in ((h, m), (24 + h, l)):
            for piece in range(3 if first == h else 2):
                stats = jnp.where(lane == first + 8 * piece, value, stats)
                value = value - value.astype(jnp.bfloat16).astype(jnp.float32)
    blended.append(stats)
    for dz in range(SIDE):
        for dy in range(SIDE):
            i = dz * SIDE + dy
            there = ((z + SIDE - dz) % SIDE) * SIDE + (y + SIDE - dy) % SIDE
            for c, part in enumerate(blended):
                cols = slice(c * HD, (c + 1) * HD)
                out[there, 0:8, cols] = part[i * 8 : (i + 1) * 8].astype(jnp.bfloat16)
                begin = image_rows + i * 8
                out[i, 8:16, cols] = part[begin : begin + 8].astype(jnp.bfloat16)


def combine_kernel(got, image_out, text_out):
    heads = (got.shape[2] - HD) // HD
    width = heads * HD
    half = image_out.shape[0]
    for y in range(SIDE):
        stats = [got[z * SIDE + y, :, width:].astype(jnp.float32) for z in range(SIDE)]
        peaks = [s + pltpu.roll(s, HD - 8, 1) + pltpu.roll(s, HD - 16, 1) for s in stats]
        sums = [pltpu.roll(s, HD - 24, 1) + pltpu.roll(s, HD - 32, 1) for s in stats]
        top = peaks[0]
        for p in peaks[1:]:
            top = jnp.maximum(top, p)
        factors = [jnp.exp(p - top) for p in peaks]
        total = 0.0
        for s, f in zip(sums, factors):
            total = total + f * s
        for h in range(heads):
            inverse = 1.0 / total[:, h : h + 1]
            acc = 0.0
            for z in range(SIDE):
                part = got[z * SIDE + y, :, h * HD : (h + 1) * HD].astype(jnp.float32)
                acc = acc + part * (factors[z][:, h : h + 1] * inverse)
            cols = slice(y * width + h * HD, y * width + (h + 1) * HD)
            image_out[:, cols] = acc[:half].astype(jnp.bfloat16)
            text_out[:, cols] = acc[half:].astype(jnp.bfloat16)


def local(
    image_query,
    image_key,
    image_value,
    text_query,
    text_key,
    text_value,
    image_query_gain,
    image_key_gain,
    text_query_gain,
    text_key_gain,
    image_order,
    text_length,
):
    rows, model = image_query.shape
    heads = model // HD
    width = model // SIDE
    text_rows = text_query.shape[0]
    block = text_rows // SIDE
    half = rows * SIDE**3 // 2
    bf, f32 = jnp.bfloat16, jnp.float32
    struct = jax.ShapeDtypeStruct
    gains = [g.reshape(1, HD) for g in (image_query_gain, image_key_gain, text_query_gain, text_key_gain)]

    own = pl.pallas_call(
        lambda *refs: prep_kernel(heads, half, *refs),
        out_shape=[pltpu.VMEM((rows, 3 * width), bf)] * SIDE,
        in_specs=[ANY] * 7,
        out_specs=[VM] * SIDE,
        scratch_shapes=[
            pltpu.SMEM((rows,), jnp.int32),
            pltpu.VMEM((1, HD), f32),
            pltpu.VMEM((rows, model), bf),
            pltpu.VMEM((rows, model), bf),
            pltpu.VMEM((rows, model), bf),
            pltpu.VMEM((1, HD), f32),
            pltpu.VMEM((1, HD), f32),
            pltpu.VMEM((rows, model), bf),
            pltpu.VMEM((rows, model), bf),
            pltpu.SemaphoreType.DMA((7,)),
        ],
        name="prep",
    )(image_order, jnp.asarray(frequencies()), image_query, image_key, image_value, gains[0], gains[1])

    from_y = [own[0]] + [shift(own[d], dy=d) for d in range(1, SIDE)]

    qt, kt, vt, bias = pl.pallas_call(
        text_kernel,
        out_shape=[pltpu.VMEM((block, width), bf)] * 3 + [pltpu.VMEM((8, block), f32)],
        in_specs=[ANY] * 6,
        out_specs=[VM] * 4,
        scratch_shapes=[
            pltpu.SMEM((1,), jnp.int32),
            pltpu.VMEM((block, width), bf),
            pltpu.VMEM((block, width), bf),
            pltpu.VMEM((1, HD), f32),
            pltpu.VMEM((1, HD), f32),
            pltpu.SemaphoreType.DMA((6,)),
        ],
        cost_estimate=pl.CostEstimate(flops=20_000_000, bytes_accessed=600_000, transcendentals=0),
        name="text",
    )(text_query, text_key, text_value, gains[2], gains[3], text_length)

    kv, q = pl.pallas_call(
        pack_kernel,
        out_shape=[pltpu.VMEM((SIDE * rows, 2 * width), bf), pltpu.VMEM((SIDE * rows, width), bf)],
        in_specs=[VM] * SIDE + [VM],
        out_specs=[VM] * 2,
        name="pack",
    )(*from_y, bias)

    kvs = [kv] + [shift(kv, dx=d) for d in range(1, SIDE)]
    qs = [q] + [shift(q, dz=d) for d in range(1, SIDE)]

    parts = SIDE * SIDE
    out_rows = rows + text_rows // SIDE**3
    partial = pl.pallas_call(
        attend_kernel,
        out_shape=pltpu.VMEM((parts, out_rows, width + HD), bf),
        in_specs=[VM] * 12,
        out_specs=VM,
        name="attend",
    )(*kvs, *qs, qt, kt, vt, bias)

    groups = [[x * parts + i for i in range(parts)] for x in range(SIDE)]
    got = in_vmem(lax.all_to_all(partial, "seq", 0, 0, axis_index_groups=groups, tiled=True))

    return pl.pallas_call(
        combine_kernel,
        out_shape=[struct((rows, model), bf), struct((out_rows - rows, model), bf)],
        in_specs=[VM],
        out_specs=[VM] * 2,
        name="combine",
    )(got)


def solution(mesh):
    token = P(("req", "seq"), None)
    text = P("req", None)
    return jax.shard_map(
        lambda *args: tuple(local(*args)),
        mesh=mesh,
        in_specs=(token, token, token, text, text, text, P(), P(), P(), P(), P(("req", "seq")), P("req")),
        out_specs=(token, token),
        check_vma=False,
    )
```

time: 49 us -> 44.3 us (0.904)
  Pallas kernels: 11.5 us -> 7.36 us
  blocking collectives: 14.1 us -> 12 us
  local copies, waits for them, and re-layouts: 1.22 us -> 3.13 us
  other arithmetic: 0.61 us -> 0 us
    pallas_call x3, Pallas kernels: 6.62 us -> 3.83 us  [the longest x1 1.85 us: local(): pl.pallas_call(attend_kernel, out_shape=pltpu.VMEM((parts, out_rows, widt...]
    all_to_all x1, blocking collectives: 14.1 us -> 12 us  [local(): lax.all_to_all(partial, 'seq', 0, 0, axis_index_groups=groups, tiled=True)]
    unnamed x18 -> x14, local copies, waits for them, and re-layouts: 1.22 us -> 3.13 us
    pallas_call x1, Pallas kernels: 1.93 us -> 1.12 us  [local(): pl.pallas_call(combine_kernel, out_shape=[struct((rows, model), bf), stru...]
    another operation x1 -> x0, other arithmetic: 0.61 us -> none  [local(): place = jnp.stack([x, z, y]).astype(jnp.int32)]
    pallas_call x1, Pallas kernels: 2.97 us -> 2.4 us  [local(): pl.pallas_call(lambda *refs: prep_kernel(heads, half, *refs), out_shape=[...]
  transfers between devices with their start and end apart: 9 -> 9, of which waited for: 3 -> 1; matrix products, arithmetic and copies ran while one was open for 0% -> 0% of each run, Pallas kernels for 5% -> 3%
where the time goes in v2:
time: 44.3 us; the launch traced here: 43.7 us
  starting transfers between devices  15.7 us (35%)
  blocking collectives  12 us (27%)
  Pallas kernels  7.36 us (17%)
  waiting for transfers between devices  4.09 us (9%)
  local copies, waits for them, and re-layouts  3.13 us (7%)
  between operations  1.38 us (3%)
    ppermute x9, starting transfers between devices, shift(): return in_vmem(lax.ppermute(value, 'seq', pairs))  15.7 us
    all_to_all x1, blocking collectives, local(): lax.all_to_all(partial, 'seq', 0, 0, axis_index_groups=groups, tiled=True)  12 us
    ppermute x9, waiting for transfers between devices, shift(): return in_vmem(lax.ppermute(value, 'seq', pairs))  4.09 us
    unnamed x14, local copies, waits for them, and re-layouts  3.13 us
    pallas_call x1, Pallas kernels, local(): pl.pallas_call(lambda *refs: prep_kernel(heads, half, *refs), out_shape=[...  2.4 us
    pallas_call x1, Pallas kernels, local(): pl.pallas_call(attend_kernel, out_shape=pltpu.VMEM((parts, out_rows, widt...  1.85 us
    pallas_call x1, Pallas kernels, local(): pl.pallas_call(text_kernel, out_shape=[pltpu.VMEM((block, width), bf)] *...  1.26 us
    pallas_call x1, Pallas kernels, local(): pl.pallas_call(combine_kernel, out_shape=[struct((rows, model), bf), stru...  1.12 us
  transfers between devices with their start and end apart: 9, of which 1 were waited for; matrix products, arithmetic and copies ran while one was open for 0% of the time, Pallas kernels for 3%

profile of v2, /device:TPU:0, one launch (start us, length us, event | category | flops | bytes accessed | tf_op | source)
XLA Modules:
  0.0 43.7 jit_solution(9752604079210572261)
XLA Ops:
  0.6 2.4 %prep.1 = (bf16[8,1152]{1,0:T(8,128)(2,1)S(1)}, bf16[8,1152]{1,0:T(8,128)(2,1)S(1)}, bf16[8,1152]{1,0:T(8,128)(2,1)S(1)}, bf16[8,1152]{1,0:T(8,128)(2,1)S(1)}) custom-call(s32[8]{0:T(128)} %refs_0_.1, f32[1,128]{1,0:T(1,128)} %constant.2.clone.refs_1_, bf16[8,1536]{1,0:T(8,128)(2,1)} %refs_2_.1, bf16[8,1536]{1,0:T(8,128)(2,1)} %refs_3_.1, ...), custom_call_target="tpu_custom_call" | custom-call | tf_op jit(solution)/shard_map/prep/pallas_call | solution.py:224
  3.0 0.0 copy-start.5
  3.1 0.6 %copy-done.5 = bf16[8,1152]{1,0:T(8,128)(2,1)} copy-done((bf16[8,1152]{1,0:T(8,128)(2,1)}, bf16[8,1152]{1,0:T(8,128)(2,1)S(1)}, u32[]{:S(2)}) %copy-start.5) | copy-done | bytes 18456
  3.7 1.7 %collective-permute-start = (bf16[8,1152]{1,0:T(8,128)(2,1)S(1)}, bf16[8,1152]{1,0:T(8,128)(2,1)S(1)}, u32[]{:S(2)}, u32[]{:S(2)}) collective-permute-start(bf16[8,1152]{1,0:T(8,128)(2,1)S(1)} %get-tuple-element.13), channel_id=1, source_target_pairs={{0,1},{1,2},{2,3},{3,0},{4,5},{5,6},{6,7},{7,4},{8,9},{9,10},{10,1... | collective-permute-start | bytes 55304 | tf_op jit(solution)/shard_map/ppermute | solution.py:34
  5.3 2.9 %collective-permute-start.1 = (bf16[8,1152]{1,0:T(8,128)(2,1)S(1)}, bf16[8,1152]{1,0:T(8,128)(2,1)S(1)}, u32[]{:S(2)}, u32[]{:S(2)}) collective-permute-start(bf16[8,1152]{1,0:T(8,128)(2,1)S(1)} %get-tuple-element.14), channel_id=1, source_target_pairs={{0,2},{1,3},{2,0},{3,1},{4,6},{5,7},{6,4},{7,5},{8,10},{9,11},{10,... | collective-permute-start | bytes 55304 | tf_op jit(solution)/shard_map/ppermute | solution.py:34
  8.2 1.3 %collective-permute-start.2 = (bf16[8,1152]{1,0:T(8,128)(2,1)S(1)}, bf16[8,1152]{1,0:T(8,128)(2,1)S(1)}, u32[]{:S(2)}, u32[]{:S(2)}) collective-permute-start(bf16[8,1152]{1,0:T(8,128)(2,1)S(1)} %get-tuple-element.15), channel_id=1, source_target_pairs={{0,3},{1,0},{2,1},{3,2},{4,7},{5,4},{6,5},{7,6},{8,11},{9,8},{10,9... | collective-permute-start | bytes 55304 | tf_op jit(solution)/shard_map/ppermute | solution.py:34
  10.2 1.3 %text.1 = (bf16[128,384]{1,0:T(8,128)(2,1)S(1)}, bf16[128,384]{1,0:T(8,128)(2,1)S(1)}, bf16[128,384]{1,0:T(8,128)(2,1)S(1)}, f32[8,128]{1,0:T(8,128)S(1)}) custom-call(bf16[512,1536]{1,0:T(8,128)(2,1)} %q_h.1, bf16[512,1536]{1,0:T(8,128)(2,1)} %k_h.1, bf16[512,1536]{1,0:T(8,128)(2,1)} %v_h.1, f32[1,128]{1,0:T(1,128)} %bitcast.6, f32[1,128]{1,0:T(1,128)} %bitcast.7, ...), custom_call_target="tpu_custom_call" | custom-call | flops 20000000 | bytes 600000 | tf_op jit(solution)/shard_map/text/pallas_call | solution.py:246
  11.5 0.6 %copy-done = bf16[128,384]{1,0:T(8,128)(2,1)} copy-done((bf16[128,384]{1,0:T(8,128)(2,1)}, bf16[128,384]{1,0:T(8,128)(2,1)S(1)}, u32[]{:S(2)}) %copy-start) | copy-done | bytes 98328
  12.2 0.6 %copy-done.1 = bf16[128,384]{1,0:T(8,128)(2,1)} copy-done((bf16[128,384]{1,0:T(8,128)(2,1)}, bf16[128,384]{1,0:T(8,128)(2,1)S(1)}, u32[]{:S(2)}) %copy-start.1) | copy-done | bytes 98328
  12.8 0.6 %copy-done.2 = bf16[128,384]{1,0:T(8,128)(2,1)} copy-done((bf16[128,384]{1,0:T(8,128)(2,1)}, bf16[128,384]{1,0:T(8,128)(2,1)S(1)}, u32[]{:S(2)}) %copy-start.2) | copy-done | bytes 98328
  13.4 0.6 %copy-done.6 = f32[8,128]{1,0:T(8,128)} copy-done((f32[8,128]{1,0:T(8,128)}, f32[8,128]{1,0:T(8,128)S(1)}, u32[]{:S(2)}) %copy-start.6) | copy-done | bytes 4120
  14.0 0.0 collective-permute-done.a1
  14.0 0.0 collective-permute-done.1.a2
  14.0 0.7 %pack.1 = (bf16[32,768]{1,0:T(8,128)(2,1)S(1)}, bf16[32,384]{1,0:T(8,128)(2,1)S(1)}) custom-call(bf16[8,1152]{1,0:T(8,128)(2,1)} %copy-done.5, bf16[8,1152]{1,0:T(8,128)(2,1)S(1)} %collective-permute-done.a1, bf16[8,1152]{1,0:T(8,128)(2,1)S(1)} %collective-permute-done.1.a2, bf16[8,1152]{1,0:T(8,128)(2,1)S(1)} %collective-permute-done.2.a3, f32[8,128]{1,0:T(8,128)} %copy-done.6), custom_call_target="tpu_custom_call" | custom-call | tf_op jit(solution)/shard_map/pack/pallas_call | solution.py:263
  14.8 0.0 copy-start.4
  14.8 4.1 %collective-permute-start.8 = (bf16[32,384]{1,0:T(8,128)(2,1)S(1)}, bf16[32,384]{1,0:T(8,128)(2,1)S(1)}, u32[]{:S(2)}, u32[]{:S(2)}) collective-permute-start(bf16[32,384]{1,0:T(8,128)(2,1)S(1)} %get-tuple-element.18.q0), channel_id=1, source_target_pairs={{0,12},{1,13},{2,14},{3,15},{4,0},{5,1},{6,2},{7,3},{8,4},{9,5},{1... | collective-permute-start | bytes 73736 | tf_op jit(solution)/shard_map/ppermute | solution.py:34
  18.9 2.8 %collective-permute-start.5 = (bf16[32,768]{1,0:T(8,128)(2,1)S(1)}, bf16[32,768]{1,0:T(8,128)(2,1)S(1)}, u32[]{:S(2)}, u32[]{:S(2)}) collective-permute-start(bf16[32,768]{1,0:T(8,128)(2,1)S(1)} %get-tuple-element.17.kv0), channel_id=1, source_target_pairs={{0,48},{1,49},{2,50},{3,51},{4,52},{5,53},{6,54},{7,55},{8,56},{9,... | collective-permute-start | bytes 147464 | tf_op jit(solution)/shard_map/ppermute | solution.py:34
  21.7 0.8 %collective-permute-start.4 = (bf16[32,768]{1,0:T(8,128)(2,1)S(1)}, bf16[32,768]{1,0:T(8,128)(2,1)S(1)}, u32[]{:S(2)}, u32[]{:S(2)}) collective-permute-start(bf16[32,768]{1,0:T(8,128)(2,1)S(1)} %get-tuple-element.17.kv0), channel_id=1, source_target_pairs={{0,32},{1,33},{2,34},{3,35},{4,36},{5,37},{6,38},{7,39},{8,40},{9,... | collective-permute-start | bytes 147464 | tf_op jit(solution)/shard_map/ppermute | solution.py:34
  22.5 0.9 %collective-permute-start.3 = (bf16[32,768]{1,0:T(8,128)(2,1)S(1)}, bf16[32,768]{1,0:T(8,128)(2,1)S(1)}, u32[]{:S(2)}, u32[]{:S(2)}) collective-permute-start(bf16[32,768]{1,0:T(8,128)(2,1)S(1)} %get-tuple-element.17.kv0), channel_id=1, source_target_pairs={{0,16},{1,17},{2,18},{3,19},{4,20},{5,21},{6,22},{7,23},{8,24},{9,... | collective-permute-start | bytes 147464 | tf_op jit(solution)/shard_map/ppermute | solution.py:34
  23.4 1.3 %collective-permute-start.6 = (bf16[32,384]{1,0:T(8,128)(2,1)S(1)}, bf16[32,384]{1,0:T(8,128)(2,1)S(1)}, u32[]{:S(2)}, u32[]{:S(2)}) collective-permute-start(bf16[32,384]{1,0:T(8,128)(2,1)S(1)} %get-tuple-element.18.q0), channel_id=1, source_target_pairs={{0,4},{1,5},{2,6},{3,7},{4,8},{5,9},{6,10},{7,11},{8,12},{9,13},{1... | collective-permute-start | bytes 73736 | tf_op jit(solution)/shard_map/ppermute | solution.py:34
  24.6 4.1 %collective-permute-done.7.q2 = bf16[32,384]{1,0:T(8,128)(2,1)S(1)} collective-permute-done((bf16[32,384]{1,0:T(8,128)(2,1)S(1)}, bf16[32,384]{1,0:T(8,128)(2,1)S(1)}, u32[]{:S(2)}, u32[]{:S(2)}) %collective-permute-start.7) | collective-permute-done | bytes 24608 | tf_op jit(solution)/shard_map/ppermute | solution.py:34
  28.7 1.8 %attend.1 = bf16[16,16,512]{2,1,0:T(8,128)(2,1)S(1)} custom-call(bf16[32,768]{1,0:T(8,128)(2,1)} %copy-done.3, bf16[32,768]{1,0:T(8,128)(2,1)S(1)} %collective-permute-done.3.kv1, bf16[32,768]{1,0:T(8,128)(2,1)S(1)} %collective-permute-done.4.kv2, bf16[32,768]{1,0:T(8,128)(2,1)S(1)} %collective-permute-done.5.kv3, bf16[32,384]{1,0:T(8,128)(2,1)} %copy-done.4, ...), custom_call_target="tpu_custom_call" | custom-call | tf_op jit(solution)/shard_map/attend/pallas_call | solution.py:276
  30.6 12.0 %all_to_all.5.got = bf16[16,16,512]{2,1,0:T(8,128)(2,1)S(1)} all-to-all(bf16[16,16,512]{2,1,0:T(8,128)(2,1)S(1)} %attend.1), channel_id=1, replica_groups={{0,1,2,3,4,5,6,7,8,9,10,11,12,13,14,15},{16,17,18,19,20,21,22,23,24,25,..., dimensions={0} | all-to-all | bytes 524288 | tf_op jit(solution)/shard_map/all_to_all | solution.py:285
  42.6 1.1 %combine.1 = (bf16[8,1536]{1,0:T(8,128)(2,1)}, bf16[8,1536]{1,0:T(8,128)(2,1)}) custom-call(bf16[16,16,512]{2,1,0:T(8,128)(2,1)S(1)} %all_to_all.5.got), custom_call_target="tpu_custom_call" | custom-call | tf_op jit(solution)/shard_map/combine/pallas_call | solution.py:287
  (14 shorter events, 0.0 us)
Async XLA Ops:
  3.0 0.6 %copy-start.5 = (bf16[8,1152]{1,0:T(8,128)(2,1)}, bf16[8,1152]{1,0:T(8,128)(2,1)S(1)}, u32[]{:S(2)}) copy-start(bf16[8,1152]{1,0:T(8,128)(2,1)S(1)} %get-tuple-element.12.a0) | copy-start | bytes 55300
  3.7 10.4 %collective-permute-start = (bf16[8,1152]{1,0:T(8,128)(2,1)S(1)}, bf16[8,1152]{1,0:T(8,128)(2,1)S(1)}, u32[]{:S(2)}, u32[]{:S(2)}) collective-permute-start(bf16[8,1152]{1,0:T(8,128)(2,1)S(1)} %get-tuple-element.13), channel_id=1, source_target_pairs={{0,1},{1,2},{2,3},{3,0},{4,5},{5,6},{6,7},{7,4},{8,9},{9,10},{10,1... | collective-permute-start | bytes 55304 | tf_op jit(solution)/shard_map/ppermute | solution.py:34
  5.3 8.7 %collective-permute-start.1 = (bf16[8,1152]{1,0:T(8,128)(2,1)S(1)}, bf16[8,1152]{1,0:T(8,128)(2,1)S(1)}, u32[]{:S(2)}, u32[]{:S(2)}) collective-permute-start(bf16[8,1152]{1,0:T(8,128)(2,1)S(1)} %get-tuple-element.14), channel_id=1, source_target_pairs={{0,2},{1,3},{2,0},{3,1},{4,6},{5,7},{6,4},{7,5},{8,10},{9,11},{10,... | collective-permute-start | bytes 55304 | tf_op jit(solution)/shard_map/ppermute | solution.py:34
  8.2 5.8 %collective-permute-start.2 = (bf16[8,1152]{1,0:T(8,128)(2,1)S(1)}, bf16[8,1152]{1,0:T(8,128)(2,1)S(1)}, u32[]{:S(2)}, u32[]{:S(2)}) collective-permute-start(bf16[8,1152]{1,0:T(8,128)(2,1)S(1)} %get-tuple-element.15), channel_id=1, source_target_pairs={{0,3},{1,0},{2,1},{3,2},{4,7},{5,4},{6,5},{7,6},{8,11},{9,8},{10,9... | collective-permute-start | bytes 55304 | tf_op jit(solution)/shard_map/ppermute | solution.py:34
  11.5 0.6 %copy-start = (bf16[128,384]{1,0:T(8,128)(2,1)}, bf16[128,384]{1,0:T(8,128)(2,1)S(1)}, u32[]{:S(2)}) copy-start(bf16[128,384]{1,0:T(8,128)(2,1)S(1)} %get-tuple-element.19.qt) | copy-start | bytes 294916
  12.2 0.6 %copy-start.1 = (bf16[128,384]{1,0:T(8,128)(2,1)}, bf16[128,384]{1,0:T(8,128)(2,1)S(1)}, u32[]{:S(2)}) copy-start(bf16[128,384]{1,0:T(8,128)(2,1)S(1)} %get-tuple-element.20.kt) | copy-start | bytes 294916
  12.8 0.6 %copy-start.2 = (bf16[128,384]{1,0:T(8,128)(2,1)}, bf16[128,384]{1,0:T(8,128)(2,1)S(1)}, u32[]{:S(2)}) copy-start(bf16[128,384]{1,0:T(8,128)(2,1)S(1)} %get-tuple-element.21.vt) | copy-start | bytes 294916
  13.4 0.6 %copy-start.6 = (f32[8,128]{1,0:T(8,128)}, f32[8,128]{1,0:T(8,128)S(1)}, u32[]{:S(2)}) copy-start(f32[8,128]{1,0:T(8,128)S(1)} %get-tuple-element.16.order_only.bias) | copy-start | bytes 12292
  14.8 13.9 %copy-start.3 = (bf16[32,768]{1,0:T(8,128)(2,1)}, bf16[32,768]{1,0:T(8,128)(2,1)S(1)}, u32[]{:S(2)}) copy-start(bf16[32,768]{1,0:T(8,128)(2,1)S(1)} %get-tuple-element.17.kv0) | copy-start | bytes 147460
  14.8 13.9 %copy-start.4 = (bf16[32,384]{1,0:T(8,128)(2,1)}, bf16[32,384]{1,0:T(8,128)(2,1)S(1)}, u32[]{:S(2)}) copy-start(bf16[32,384]{1,0:T(8,128)(2,1)S(1)} %get-tuple-element.18.q0) | copy-start | bytes 73732
  14.8 8.6 %collective-permute-start.8 = (bf16[32,384]{1,0:T(8,128)(2,1)S(1)}, bf16[32,384]{1,0:T(8,128)(2,1)S(1)}, u32[]{:S(2)}, u32[]{:S(2)}) collective-permute-start(bf16[32,384]{1,0:T(8,128)(2,1)S(1)} %get-tuple-element.18.q0), channel_id=1, source_target_pairs={{0,12},{1,13},{2,14},{3,15},{4,0},{5,1},{6,2},{7,3},{8,4},{9,5},{1... | collective-permute-start | bytes 73736 | tf_op jit(solution)/shard_map/ppermute | solution.py:34
  18.9 9.8 %collective-permute-start.5 = (bf16[32,768]{1,0:T(8,128)(2,1)S(1)}, bf16[32,768]{1,0:T(8,128)(2,1)S(1)}, u32[]{:S(2)}, u32[]{:S(2)}) collective-permute-start(bf16[32,768]{1,0:T(8,128)(2,1)S(1)} %get-tuple-element.17.kv0), channel_id=1, source_target_pairs={{0,48},{1,49},{2,50},{3,51},{4,52},{5,53},{6,54},{7,55},{8,56},{9,... | collective-permute-start | bytes 147464 | tf_op jit(solution)/shard_map/ppermute | solution.py:34
  21.7 7.0 %collective-permute-start.4 = (bf16[32,768]{1,0:T(8,128)(2,1)S(1)}, bf16[32,768]{1,0:T(8,128)(2,1)S(1)}, u32[]{:S(2)}, u32[]{:S(2)}) collective-permute-start(bf16[32,768]{1,0:T(8,128)(2,1)S(1)} %get-tuple-element.17.kv0), channel_id=1, source_target_pairs={{0,32},{1,33},{2,34},{3,35},{4,36},{5,37},{6,38},{7,39},{8,40},{9,... | collective-permute-start | bytes 147464 | tf_op jit(solution)/shard_map/ppermute | solution.py:34
  22.5 6.2 %collective-permute-start.3 = (bf16[32,768]{1,0:T(8,128)(2,1)S(1)}, bf16[32,768]{1,0:T(8,128)(2,1)S(1)}, u32[]{:S(2)}, u32[]{:S(2)}) collective-permute-start(bf16[32,768]{1,0:T(8,128)(2,1)S(1)} %get-tuple-element.17.kv0), channel_id=1, source_target_pairs={{0,16},{1,17},{2,18},{3,19},{4,20},{5,21},{6,22},{7,23},{8,24},{9,... | collective-permute-start | bytes 147464 | tf_op jit(solution)/shard_map/ppermute | solution.py:34
  23.3 5.3 %collective-permute-start.7 = (bf16[32,384]{1,0:T(8,128)(2,1)S(1)}, bf16[32,384]{1,0:T(8,128)(2,1)S(1)}, u32[]{:S(2)}, u32[]{:S(2)}) collective-permute-start(bf16[32,384]{1,0:T(8,128)(2,1)S(1)} %get-tuple-element.18.q0), channel_id=1, source_target_pairs={{0,8},{1,9},{2,10},{3,11},{4,12},{5,13},{6,14},{7,15},{8,0},{9,1},... | collective-permute-start | bytes 73736 | tf_op jit(solution)/shard_map/ppermute | solution.py:34
  23.4 5.3 %collective-permute-start.6 = (bf16[32,384]{1,0:T(8,128)(2,1)S(1)}, bf16[32,384]{1,0:T(8,128)(2,1)S(1)}, u32[]{:S(2)}, u32[]{:S(2)}) collective-permute-start(bf16[32,384]{1,0:T(8,128)(2,1)S(1)} %get-tuple-element.18.q0), channel_id=1, source_target_pairs={{0,4},{1,5},{2,6},{3,7},{4,8},{5,9},{6,10},{7,11},{8,12},{9,13},{1... | collective-permute-start | bytes 73736 | tf_op jit(solution)/shard_map/ppermute | solution.py:34

commit v3 on v2

--- a/solution.py
+++ b/solution.py
@@ -15,7 +15,7 @@
 
 VM = pl.BlockSpec(memory_space=pltpu.VMEM)
 SM = pl.BlockSpec(memory_space=pltpu.SMEM)
-ANY = pl.BlockSpec(memory_space=pl.ANY)
+HB = pl.BlockSpec(memory_space=pltpu.HBM)
 
 
 def split_index(i):
@@ -36,6 +36,11 @@
 
 def in_vmem(value):
     return pltpu.with_memory_space_constraint(value, pltpu.VMEM)
+
+
+def vmem_call(kernel, **options):
+    call = pl.pallas_call(kernel, **options)
+    return lambda *args: jax.tree.map(in_vmem, call(*args))
 
 
 def head_norm(x, gain):
@@ -221,10 +226,10 @@
     struct = jax.ShapeDtypeStruct
     gains = [g.reshape(1, HD) for g in (image_query_gain, image_key_gain, text_query_gain, text_key_gain)]
 
-    own = pl.pallas_call(
+    own = vmem_call(
         lambda *refs: prep_kernel(heads, half, *refs),
         out_shape=[pltpu.VMEM((rows, 3 * width), bf)] * SIDE,
-        in_specs=[ANY] * 7,
+        in_specs=[HB] * 7,
         out_specs=[VM] * SIDE,
         scratch_shapes=[
             pltpu.SMEM((rows,), jnp.int32),
@@ -243,10 +248,10 @@
 
     from_y = [own[0]] + [shift(own[d], dy=d) for d in range(1, SIDE)]
 
-    qt, kt, vt, bias = pl.pallas_call(
+    qt, kt, vt, bias = vmem_call(
         text_kernel,
         out_shape=[pltpu.VMEM((block, width), bf)] * 3 + [pltpu.VMEM((8, block), f32)],
-        in_specs=[ANY] * 6,
+        in_specs=[HB] * 6,
         out_specs=[VM] * 4,
         scratch_shapes=[
             pltpu.SMEM((1,), jnp.int32),
@@ -260,7 +265,7 @@
         name="text",
     )(text_query, text_key, text_value, gains[2], gains[3], text_length)
 
-    kv, q = pl.pallas_call(
+    kv, q = vmem_call(
         pack_kernel,
         out_shape=[pltpu.VMEM((SIDE * rows, 2 * width), bf), pltpu.VMEM((SIDE * rows, width), bf)],
         in_specs=[VM] * SIDE + [VM],

time: 44.3 us -> 41.6 us (0.939)
  local copies, waits for them, and re-layouts: 3.13 us -> 0 us
  blocking collectives: 12 us -> 13.9 us
  Pallas kernels: 7.36 us -> 5.6 us
  waiting for transfers between devices: 4.09 us -> 4.56 us
    unnamed x14 -> x0, local copies, waits for them, and re-layouts: 3.13 us -> none
    all_to_all x1, blocking collectives: 12 us -> 13.9 us  [local(): lax.all_to_all(partial, 'seq', 0, 0, axis_index_groups=groups, tiled=True)]
    pallas_call x1, Pallas kernels: 1.85 us -> 0.81 us  [local(): pl.pallas_call(attend_kernel, out_shape=pltpu.VMEM((parts, out_rows, widt...]
    pallas_call x3, Pallas kernels: 4.39 us -> 3.67 us  [vmem_call(): return lambda *args: jax.tree.map(in_vmem, call(*args))]
    ppermute x9, waiting for transfers between devices: 4.09 us -> 4.56 us  [shift(): return in_vmem(lax.ppermute(value, 'seq', pairs))]
  transfers between devices with their start and end apart: 9 -> 9, of which waited for: 1 -> 2; matrix products, arithmetic and copies ran while one was open for 0% -> 0% of each run, Pallas kernels for 3% -> 3%
where the time goes in v3:
time: 41.6 us; the launch traced here: 41.1 us
  starting transfers between devices  15.7 us (38%)
  blocking collectives  13.9 us (33%)
  Pallas kernels  5.6 us (13%)
  waiting for transfers between devices  4.56 us (11%)
  between operations  1.34 us (3%)
    ppermute x9, starting transfers between devices, shift(): return in_vmem(lax.ppermute(value, 'seq', pairs))  15.7 us
    all_to_all x1, blocking collectives, local(): lax.all_to_all(partial, 'seq', 0, 0, axis_index_groups=groups, tiled=True)  13.9 us
    ppermute x9, waiting for transfers between devices, shift(): return in_vmem(lax.ppermute(value, 'seq', pairs))  4.56 us
    pallas_call x3, Pallas kernels, vmem_call(): return lambda *args: jax.tree.map(in_vmem, call(*args))  3.67 us
    pallas_call x1, Pallas kernels, local(): pl.pallas_call(combine_kernel, out_shape=[struct((rows, model), bf), stru...  1.12 us
  transfers between devices with their start and end apart: 9, of which 2 were waited for; matrix products, arithmetic and copies ran while one was open for 0% of the time, Pallas kernels for 3%

profile of v3, /device:TPU:0, one launch (start us, length us, event | category | flops | bytes accessed | tf_op | source)
XLA Modules:
  0.0 41.1 jit_solution(17570683484869502708)
XLA Ops:
  0.6 2.4 %prep.1 = (bf16[8,1152]{1,0:T(8,128)(2,1)S(1)}, bf16[8,1152]{1,0:T(8,128)(2,1)S(1)}, bf16[8,1152]{1,0:T(8,128)(2,1)S(1)}, bf16[8,1152]{1,0:T(8,128)(2,1)S(1)}) custom-call(s32[8]{0:T(128)} %refs_0_.1, f32[1,128]{1,0:T(1,128)} %constant.2.clone.refs_1_, bf16[8,1536]{1,0:T(8,128)(2,1)} %refs_2_.1, bf16[8,1536]{1,0:T(8,128)(2,1)} %refs_3_.1, ...), custom_call_target="tpu_custom_call" | custom-call | tf_op jit(solution)/shard_map/prep/pallas_call | solution.py:43
  3.0 1.8 %collective-permute-start = (bf16[8,1152]{1,0:T(8,128)(2,1)S(1)}, bf16[8,1152]{1,0:T(8,128)(2,1)S(1)}, u32[]{:S(2)}, u32[]{:S(2)}) collective-permute-start(bf16[8,1152]{1,0:T(8,128)(2,1)S(1)} %get-tuple-element.13), channel_id=1, source_target_pairs={{0,1},{1,2},{2,3},{3,0},{4,5},{5,6},{6,7},{7,4},{8,9},{9,10},{10,1... | collective-permute-start | bytes 55304 | tf_op jit(solution)/shard_map/ppermute | solution.py:34
  4.8 2.9 %collective-permute-start.1 = (bf16[8,1152]{1,0:T(8,128)(2,1)S(1)}, bf16[8,1152]{1,0:T(8,128)(2,1)S(1)}, u32[]{:S(2)}, u32[]{:S(2)}) collective-permute-start(bf16[8,1152]{1,0:T(8,128)(2,1)S(1)} %get-tuple-element.14), channel_id=1, source_target_pairs={{0,2},{1,3},{2,0},{3,1},{4,6},{5,7},{6,4},{7,5},{8,10},{9,11},{10,... | collective-permute-start | bytes 55304 | tf_op jit(solution)/shard_map/ppermute | solution.py:34
  7.7 1.3 %collective-permute-start.2 = (bf16[8,1152]{1,0:T(8,128)(2,1)S(1)}, bf16[8,1152]{1,0:T(8,128)(2,1)S(1)}, u32[]{:S(2)}, u32[]{:S(2)}) collective-permute-start(bf16[8,1152]{1,0:T(8,128)(2,1)S(1)} %get-tuple-element.15), channel_id=1, source_target_pairs={{0,3},{1,0},{2,1},{3,2},{4,7},{5,4},{6,5},{7,6},{8,11},{9,8},{10,9... | collective-permute-start | bytes 55304 | tf_op jit(solution)/shard_map/ppermute | solution.py:34
  9.7 1.3 %text.1 = (bf16[128,384]{1,0:T(8,128)(2,1)S(1)}, bf16[128,384]{1,0:T(8,128)(2,1)S(1)}, bf16[128,384]{1,0:T(8,128)(2,1)S(1)}, f32[8,128]{1,0:T(8,128)S(1)}) custom-call(bf16[512,1536]{1,0:T(8,128)(2,1)} %q_h.1, bf16[512,1536]{1,0:T(8,128)(2,1)} %k_h.1, bf16[512,1536]{1,0:T(8,128)(2,1)} %v_h.1, f32[1,128]{1,0:T(1,128)} %bitcast.6, f32[1,128]{1,0:T(1,128)} %bitcast.7, ...), custom_call_target="tpu_custom_call" | custom-call | flops 20000000 | bytes 600000 | tf_op jit(solution)/shard_map/text/pallas_call | solution.py:43
  11.0 0.0 collective-permute-done.a1
  11.0 0.0 collective-permute-done.1.a2
  11.0 0.5 %collective-permute-done.2.a3 = bf16[8,1152]{1,0:T(8,128)(2,1)S(1)} collective-permute-done((bf16[8,1152]{1,0:T(8,128)(2,1)S(1)}, bf16[8,1152]{1,0:T(8,128)(2,1)S(1)}, u32[]{:S(2)}, u32[]{:S(2)}) %collective-permute-start.2) | collective-permute-done | bytes 18464 | tf_op jit(solution)/shard_map/ppermute | solution.py:34
  11.5 4.0 %collective-permute-start.8 = (bf16[32,384]{1,0:T(8,128)(2,1)S(1)}, bf16[32,384]{1,0:T(8,128)(2,1)S(1)}, u32[]{:S(2)}, u32[]{:S(2)}) collective-permute-start(bf16[32,384]{1,0:T(8,128)(2,1)S(1)} %get-tuple-element.18.q0), channel_id=1, source_target_pairs={{0,12},{1,13},{2,14},{3,15},{4,0},{5,1},{6,2},{7,3},{8,4},{9,5},{1... | collective-permute-start | bytes 73736 | tf_op jit(solution)/shard_map/ppermute | solution.py:34
  15.5 2.8 %collective-permute-start.5 = (bf16[32,768]{1,0:T(8,128)(2,1)S(1)}, bf16[32,768]{1,0:T(8,128)(2,1)S(1)}, u32[]{:S(2)}, u32[]{:S(2)}) collective-permute-start(bf16[32,768]{1,0:T(8,128)(2,1)S(1)} %get-tuple-element.17.kv0), channel_id=1, source_target_pairs={{0,48},{1,49},{2,50},{3,51},{4,52},{5,53},{6,54},{7,55},{8,56},{9,... | collective-permute-start | bytes 147464 | tf_op jit(solution)/shard_map/ppermute | solution.py:34
  18.3 0.8 %collective-permute-start.4 = (bf16[32,768]{1,0:T(8,128)(2,1)S(1)}, bf16[32,768]{1,0:T(8,128)(2,1)S(1)}, u32[]{:S(2)}, u32[]{:S(2)}) collective-permute-start(bf16[32,768]{1,0:T(8,128)(2,1)S(1)} %get-tuple-element.17.kv0), channel_id=1, source_target_pairs={{0,32},{1,33},{2,34},{3,35},{4,36},{5,37},{6,38},{7,39},{8,40},{9,... | collective-permute-start | bytes 147464 | tf_op jit(solution)/shard_map/ppermute | solution.py:34
  19.1 0.9 %collective-permute-start.3 = (bf16[32,768]{1,0:T(8,128)(2,1)S(1)}, bf16[32,768]{1,0:T(8,128)(2,1)S(1)}, u32[]{:S(2)}, u32[]{:S(2)}) collective-permute-start(bf16[32,768]{1,0:T(8,128)(2,1)S(1)} %get-tuple-element.17.kv0), channel_id=1, source_target_pairs={{0,16},{1,17},{2,18},{3,19},{4,20},{5,21},{6,22},{7,23},{8,24},{9,... | collective-permute-start | bytes 147464 | tf_op jit(solution)/shard_map/ppermute | solution.py:34
  20.0 0.0 collective-permute-start.7
  20.0 0.0 collective-permute-done.8.q3
  20.0 1.3 %collective-permute-start.6 = (bf16[32,384]{1,0:T(8,128)(2,1)S(1)}, bf16[32,384]{1,0:T(8,128)(2,1)S(1)}, u32[]{:S(2)}, u32[]{:S(2)}) collective-permute-start(bf16[32,384]{1,0:T(8,128)(2,1)S(1)} %get-tuple-element.18.q0), channel_id=1, source_target_pairs={{0,4},{1,5},{2,6},{3,7},{4,8},{5,9},{6,10},{7,11},{8,12},{9,13},{1... | collective-permute-start | bytes 73736 | tf_op jit(solution)/shard_map/ppermute | solution.py:34
  21.2 4.1 %collective-permute-done.7.q2 = bf16[32,384]{1,0:T(8,128)(2,1)S(1)} collective-permute-done((bf16[32,384]{1,0:T(8,128)(2,1)S(1)}, bf16[32,384]{1,0:T(8,128)(2,1)S(1)}, u32[]{:S(2)}, u32[]{:S(2)}) %collective-permute-start.7) | collective-permute-done | bytes 24608 | tf_op jit(solution)/shard_map/ppermute | solution.py:34
  25.3 0.0 collective-permute-done.6.q1
  25.3 0.0 collective-permute-done.5.kv3
  25.3 0.0 collective-permute-done.4.kv2
  25.3 0.0 collective-permute-done.3.kv1
  25.3 0.8 %attend.1 = bf16[16,16,512]{2,1,0:T(8,128)(2,1)S(1)} custom-call(bf16[32,768]{1,0:T(8,128)(2,1)S(1)} %get-tuple-element.17.kv0, bf16[32,768]{1,0:T(8,128)(2,1)S(1)} %collective-permute-done.3.kv1, bf16[32,768]{1,0:T(8,128)(2,1)S(1)} %collective-permute-done.4.kv2, bf16[32,768]{1,0:T(8,128)(2,1)S(1)} %collective-permute-done.5.kv3, ...), custom_call_target="tpu_custom_call" | custom-call | tf_op jit(solution)/shard_map/attend/pallas_call | solution.py:281
  26.1 13.9 %all_to_all.5.got = bf16[16,16,512]{2,1,0:T(8,128)(2,1)S(1)} all-to-all(bf16[16,16,512]{2,1,0:T(8,128)(2,1)S(1)} %attend.1), channel_id=1, replica_groups={{0,1,2,3,4,5,6,7,8,9,10,11,12,13,14,15},{16,17,18,19,20,21,22,23,24,25,..., dimensions={0} | all-to-all | bytes 524288 | tf_op jit(solution)/shard_map/all_to_all | solution.py:290
  40.0 1.1 %combine.1 = (bf16[8,1536]{1,0:T(8,128)(2,1)}, bf16[8,1536]{1,0:T(8,128)(2,1)}) custom-call(bf16[16,16,512]{2,1,0:T(8,128)(2,1)S(1)} %all_to_all.5.got), custom_call_target="tpu_custom_call" | custom-call | tf_op jit(solution)/shard_map/combine/pallas_call | solution.py:292
  (1 shorter events, 0.0 us)
Async XLA Ops:
  3.0 7.9 %collective-permute-start = (bf16[8,1152]{1,0:T(8,128)(2,1)S(1)}, bf16[8,1152]{1,0:T(8,128)(2,1)S(1)}, u32[]{:S(2)}, u32[]{:S(2)}) collective-permute-start(bf16[8,1152]{1,0:T(8,128)(2,1)S(1)} %get-tuple-element.13), channel_id=1, source_target_pairs={{0,1},{1,2},{2,3},{3,0},{4,5},{5,6},{6,7},{7,4},{8,9},{9,10},{10,1... | collective-permute-start | bytes 55304 | tf_op jit(solution)/shard_map/ppermute | solution.py:34
  4.8 6.2 %collective-permute-start.1 = (bf16[8,1152]{1,0:T(8,128)(2,1)S(1)}, bf16[8,1152]{1,0:T(8,128)(2,1)S(1)}, u32[]{:S(2)}, u32[]{:S(2)}) collective-permute-start(bf16[8,1152]{1,0:T(8,128)(2,1)S(1)} %get-tuple-element.14), channel_id=1, source_target_pairs={{0,2},{1,3},{2,0},{3,1},{4,6},{5,7},{6,4},{7,5},{8,10},{9,11},{10,... | collective-permute-start | bytes 55304 | tf_op jit(solution)/shard_map/ppermute | solution.py:34
  7.7 3.8 %collective-permute-start.2 = (bf16[8,1152]{1,0:T(8,128)(2,1)S(1)}, bf16[8,1152]{1,0:T(8,128)(2,1)S(1)}, u32[]{:S(2)}, u32[]{:S(2)}) collective-permute-start(bf16[8,1152]{1,0:T(8,128)(2,1)S(1)} %get-tuple-element.15), channel_id=1, source_target_pairs={{0,3},{1,0},{2,1},{3,2},{4,7},{5,4},{6,5},{7,6},{8,11},{9,8},{10,9... | collective-permute-start | bytes 55304 | tf_op jit(solution)/shard_map/ppermute | solution.py:34
  11.5 8.5 %collective-permute-start.8 = (bf16[32,384]{1,0:T(8,128)(2,1)S(1)}, bf16[32,384]{1,0:T(8,128)(2,1)S(1)}, u32[]{:S(2)}, u32[]{:S(2)}) collective-permute-start(bf16[32,384]{1,0:T(8,128)(2,1)S(1)} %get-tuple-element.18.q0), channel_id=1, source_target_pairs={{0,12},{1,13},{2,14},{3,15},{4,0},{5,1},{6,2},{7,3},{8,4},{9,5},{1... | collective-permute-start | bytes 73736 | tf_op jit(solution)/shard_map/ppermute | solution.py:34
  15.5 9.8 %collective-permute-start.5 = (bf16[32,768]{1,0:T(8,128)(2,1)S(1)}, bf16[32,768]{1,0:T(8,128)(2,1)S(1)}, u32[]{:S(2)}, u32[]{:S(2)}) collective-permute-start(bf16[32,768]{1,0:T(8,128)(2,1)S(1)} %get-tuple-element.17.kv0), channel_id=1, source_target_pairs={{0,48},{1,49},{2,50},{3,51},{4,52},{5,53},{6,54},{7,55},{8,56},{9,... | collective-permute-start | bytes 147464 | tf_op jit(solution)/shard_map/ppermute | solution.py:34
  18.3 7.0 %collective-permute-start.4 = (bf16[32,768]{1,0:T(8,128)(2,1)S(1)}, bf16[32,768]{1,0:T(8,128)(2,1)S(1)}, u32[]{:S(2)}, u32[]{:S(2)}) collective-permute-start(bf16[32,768]{1,0:T(8,128)(2,1)S(1)} %get-tuple-element.17.kv0), channel_id=1, source_target_pairs={{0,32},{1,33},{2,34},{3,35},{4,36},{5,37},{6,38},{7,39},{8,40},{9,... | collective-permute-start | bytes 147464 | tf_op jit(solution)/shard_map/ppermute | solution.py:34
  19.1 6.2 %collective-permute-start.3 = (bf16[32,768]{1,0:T(8,128)(2,1)S(1)}, bf16[32,768]{1,0:T(8,128)(2,1)S(1)}, u32[]{:S(2)}, u32[]{:S(2)}) collective-permute-start(bf16[32,768]{1,0:T(8,128)(2,1)S(1)} %get-tuple-element.17.kv0), channel_id=1, source_target_pairs={{0,16},{1,17},{2,18},{3,19},{4,20},{5,21},{6,22},{7,23},{8,24},{9,... | collective-permute-start | bytes 147464 | tf_op jit(solution)/shard_map/ppermute | solution.py:34
  20.0 5.3 %collective-permute-start.7 = (bf16[32,384]{1,0:T(8,128)(2,1)S(1)}, bf16[32,384]{1,0:T(8,128)(2,1)S(1)}, u32[]{:S(2)}, u32[]{:S(2)}) collective-permute-start(bf16[32,384]{1,0:T(8,128)(2,1)S(1)} %get-tuple-element.18.q0), channel_id=1, source_target_pairs={{0,8},{1,9},{2,10},{3,11},{4,12},{5,13},{6,14},{7,15},{8,0},{9,1},... | collective-permute-start | bytes 73736 | tf_op jit(solution)/shard_map/ppermute | solution.py:34
  20.0 5.3 %collective-permute-start.6 = (bf16[32,384]{1,0:T(8,128)(2,1)S(1)}, bf16[32,384]{1,0:T(8,128)(2,1)S(1)}, u32[]{:S(2)}, u32[]{:S(2)}) collective-permute-start(bf16[32,384]{1,0:T(8,128)(2,1)S(1)} %get-tuple-element.18.q0), channel_id=1, source_target_pairs={{0,4},{1,5},{2,6},{3,7},{4,8},{5,9},{6,10},{7,11},{8,12},{9,13},{1... | collective-permute-start | bytes 73736 | tf_op jit(solution)/shard_map/ppermute | solution.py:34

commit v4 on v3

--- a/solution.py
+++ b/solution.py
@@ -22,15 +22,24 @@
     return i // (SIDE * SIDE), (i // SIDE) % SIDE, i % SIDE
 
 
-def join_index(x, z, y):
-    return ((x % SIDE) * SIDE + z % SIDE) * SIDE + y % SIDE
-
-
-def shift(value, dx=0, dz=0, dy=0):
+def head_group(z, y):
+    return ((z ^ (z >> 1)) & 1) * 2 + ((y ^ (y >> 1)) & 1)
+
+
+def key_group(z, y):
+    return (z >> 1) * 2 + (y >> 1)
+
+
+HEAD_STEPS = ((0, 0, 0), (0, 1, 1), (0, 1, 0), (0, 0, 1))
+QUERY_STEPS = ((0, 0, 0), (0, 3, 3), (0, 3, 0), (0, 0, 3))
+KEY_STEPS = ((0, 0, 0), (2, 0, 0), (1, 0, 0), (3, 0, 0))
+
+
+def exchange(value, step):
     pairs = []
     for i in range(SIDE**3):
         x, z, y = split_index(i)
-        pairs.append((i, join_index(x + dx, z + dz, y + dy)))
+        pairs.append((i, ((x ^ step[0]) * SIDE + (z ^ step[1])) * SIDE + (y ^ step[2])))
     return in_vmem(lax.ppermute(value, "seq", pairs))
 
 
@@ -71,32 +80,36 @@
     rows = q_in.shape[0]
     lane = lax.broadcasted_iota(jnp.int32, (rows, HD), 1)
     row = lax.broadcasted_iota(jnp.int32, (rows, HD), 0)
-    pair = lane // 2
-    t = jnp.zeros((rows, HD), jnp.int32)
-    u = t
-    w = t
+    position = jnp.zeros((rows, HD), jnp.int32)
     for i in range(rows):
-        p = order[i]
-        inside = p % half
-        t = jnp.where(row == i, p // half, t)
-        u = jnp.where(row == i, inside // GRID_W, u)
-        w = jnp.where(row == i, inside % GRID_W, w)
-    coordinate = jnp.where(pair < 8, t, jnp.where(pair < 36, u, w)).astype(jnp.float32)
-    angle = coordinate * freq[...]
+        position = jnp.where(row == i, order[i], position)
+    inside = position & (half - 1)
+    pair = lane >> 1
+    coordinate = jnp.where(
+        pair < 8,
+        position >> (half.bit_length() - 1),
+        jnp.where(pair < 36, inside >> (GRID_W.bit_length() - 1), inside & (GRID_W - 1)),
+    )
+    angle = coordinate.astype(jnp.float32) * freq[...]
     cosine = jnp.cos(angle)
     sine = jnp.sin(angle)
-    even = lane % 2 == 0
+    even = (lane & 1) == 0
     sine = jnp.where(even, -sine, sine)
-    for src, gain, dst in ((q_in, qg, q_s), (k_in, kg, k_s)):
-        g = gain[...]
-        for h in range(heads):
-            x = head_norm(src[:, h * HD : (h + 1) * HD].astype(jnp.float32), g)
-            partner = jnp.where(even, pltpu.roll(x, HD - 1, 1), pltpu.roll(x, 1, 1))
-            dst[:, h * HD : (h + 1) * HD] = (x * cosine + partner * sine).astype(jnp.bfloat16)
+    blocks = [
+        src[:, h * HD : (h + 1) * HD].astype(jnp.float32) for src in (q_in, k_in) for h in range(heads)
+    ]
+    whole = jnp.concatenate(blocks, axis=0)
+    mean_square = jnp.mean(whole * whole, axis=-1, keepdims=True)
+    whole = whole * lax.rsqrt(mean_square + EPS)
+    for n in range(2 * heads):
+        gain, dst, h = (qg, q_s, n) if n < heads else (kg, k_s, n - heads)
+        x = whole[n * rows : (n + 1) * rows] * gain[...]
+        partner = jnp.where(even, pltpu.roll(x, HD - 1, 1), pltpu.roll(x, 1, 1))
+        dst[:, h * HD : (h + 1) * HD] = (x * cosine + partner * sine).astype(jnp.bfloat16)
     width = heads // SIDE * HD
-    y = lax.axis_index("seq") % SIDE
-    for d, out in enumerate((o0, o1, o2, o3)):
-        start = pl.multiple_of(((y + d) % SIDE) * width, HD)
+    _, z, y = split_index(lax.axis_index("seq"))
+    for step, out in zip(HEAD_STEPS, (o0, o1, o2, o3)):
+        start = pl.multiple_of(head_group(z ^ step[1], y ^ step[2]) * width, HD)
         out[:, 0:width] = k_s[:, pl.ds(start, width)]
         out[:, width : 2 * width] = v_in[:, pl.ds(start, width)]
         out[:, 2 * width : 3 * width] = q_s[:, pl.ds(start, width)]
@@ -113,9 +126,10 @@
 def text_kernel(q_h, k_h, v_h, qg_h, kg_h, length_h, q_out, k_out, v_out, bias, length, q_in, k_in, qg, kg, sems):
     block, width = q_in.shape
     x, z, y = split_index(lax.axis_index("seq"))
-    cols = pl.ds(pl.multiple_of(y * width, HD), width)
+    group = key_group(z, y)
+    cols = pl.ds(pl.multiple_of(head_group(z, y) * width, HD), width)
     q_rows = pl.ds(pl.multiple_of(x * block, block), block)
-    k_rows = pl.ds(pl.multiple_of(z * block, block), block)
+    k_rows = pl.ds(pl.multiple_of(group * block, block), block)
     load(
         (
             (length_h, length),
@@ -132,7 +146,7 @@
         for h in range(width // HD):
             at = slice(h * HD, (h + 1) * HD)
             dst[:, at] = head_norm(src[:, at].astype(jnp.float32), g).astype(jnp.bfloat16)
-    key = lax.broadcasted_iota(jnp.int32, bias.shape, 1) + z * block
+    key = lax.broadcasted_iota(jnp.int32, bias.shape, 1) + group * block
     bias[...] = jnp.where(key < length[0], 0.0, MASKED)
 
 
@@ -165,10 +179,10 @@
                 stats = jnp.where(lane == first + 8 * piece, value, stats)
                 value = value - value.astype(jnp.bfloat16).astype(jnp.float32)
     blended.append(stats)
-    for dz in range(SIDE):
-        for dy in range(SIDE):
-            i = dz * SIDE + dy
-            there = ((z + SIDE - dz) % SIDE) * SIDE + (y + SIDE - dy) % SIDE
+    for a, key_step in enumerate(QUERY_STEPS):
+        for b, head_step in enumerate(HEAD_STEPS):
+            i = a * SIDE + b
+            there = (z ^ key_step[1] ^ head_step[1]) * SIDE + (y ^ key_step[2] ^ head_step[2])
             for c, part in enumerate(blended):
                 cols = slice(c * HD, (c + 1) * HD)
                 out[there, 0:8, cols] = part[i * 8 : (i + 1) * 8].astype(jnp.bfloat16)
@@ -180,26 +194,32 @@
     heads = (got.shape[2] - HD) // HD
     width = heads * HD
     half = image_out.shape[0]
-    for y in range(SIDE):
-        stats = [got[z * SIDE + y, :, width:].astype(jnp.float32) for z in range(SIDE)]
-        peaks = [s + pltpu.roll(s, HD - 8, 1) + pltpu.roll(s, HD - 16, 1) for s in stats]
-        sums = [pltpu.roll(s, HD - 24, 1) + pltpu.roll(s, HD - 32, 1) for s in stats]
-        top = peaks[0]
-        for p in peaks[1:]:
-            top = jnp.maximum(top, p)
-        factors = [jnp.exp(p - top) for p in peaks]
-        total = 0.0
-        for s, f in zip(sums, factors):
-            total = total + f * s
-        for h in range(heads):
-            inverse = 1.0 / total[:, h : h + 1]
-            acc = 0.0
-            for z in range(SIDE):
-                part = got[z * SIDE + y, :, h * HD : (h + 1) * HD].astype(jnp.float32)
-                acc = acc + part * (factors[z][:, h : h + 1] * inverse)
-            cols = slice(y * width + h * HD, y * width + (h + 1) * HD)
-            image_out[:, cols] = acc[:half].astype(jnp.bfloat16)
-            text_out[:, cols] = acc[half:].astype(jnp.bfloat16)
+    members = [[None] * SIDE for _ in range(SIDE)]
+    for z in range(SIDE):
+        for y in range(SIDE):
+            members[key_group(z, y)][head_group(z, y)] = z * SIDE + y
+
+    def stacked(key, cols):
+        return jnp.concatenate([got[m, :, cols].astype(jnp.float32) for m in members[key]], axis=0)
+
+    stats = [stacked(key, slice(width, width + HD)) for key in range(SIDE)]
+    peaks = [s + pltpu.roll(s, HD - 8, 1) + pltpu.roll(s, HD - 16, 1) for s in stats]
+    sums = [pltpu.roll(s, HD - 24, 1) + pltpu.roll(s, HD - 32, 1) for s in stats]
+    top = jnp.maximum(jnp.maximum(peaks[0], peaks[1]), jnp.maximum(peaks[2], peaks[3]))
+    factors = [jnp.exp(p - top) for p in peaks]
+    total = factors[0] * sums[0] + factors[1] * sums[1] + factors[2] * sums[2] + factors[3] * sums[3]
+    lane = lax.broadcasted_iota(jnp.int32, total.shape, 1)
+    inverse = 1.0 / jnp.where(lane < heads, total, 1.0)
+    weights = [f * inverse for f in factors]
+    for h in range(heads):
+        acc = 0.0
+        for key in range(SIDE):
+            acc = acc + stacked(key, slice(h * HD, (h + 1) * HD)) * weights[key][:, h : h + 1]
+        for g in range(SIDE):
+            cols = slice(g * width + h * HD, g * width + (h + 1) * HD)
+            rows = acc[g * 2 * half : (g + 1) * 2 * half].astype(jnp.bfloat16)
+            image_out[:, cols] = rows[:half]
+            text_out[:, cols] = rows[half:]
 
 
 def local(
@@ -246,7 +266,7 @@
         name="prep",
     )(image_order, jnp.asarray(frequencies()), image_query, image_key, image_value, gains[0], gains[1])
 
-    from_y = [own[0]] + [shift(own[d], dy=d) for d in range(1, SIDE)]
+    from_y = [own[0]] + [exchange(own[d], HEAD_STEPS[d]) for d in range(1, SIDE)]
 
     qt, kt, vt, bias = vmem_call(
         text_kernel,
@@ -273,8 +293,8 @@
         name="pack",
     )(*from_y, bias)
 
-    kvs = [kv] + [shift(kv, dx=d) for d in range(1, SIDE)]
-    qs = [q] + [shift(q, dz=d) for d in range(1, SIDE)]
+    kvs = [kv] + [exchange(kv, step) for step in KEY_STEPS[1:]]
+    qs = [q] + [exchange(q, step) for step in QUERY_STEPS[1:]]
 
     parts = SIDE * SIDE
     out_rows = rows + text_rows // SIDE**3

time: 41.6 us -> 40.1 us (0.964)
  waiting for transfers between devices: 4.56 us -> 7.94 us
  blocking collectives: 13.9 us -> 11.3 us
  Pallas kernels: 5.6 us -> 4.09 us
  starting transfers between devices: 15.7 us -> 15.2 us
    ppermute x9, waiting for transfers between devices: 4.56 us -> 7.94 us  [exchange(): return in_vmem(lax.ppermute(value, 'seq', pairs))]
    all_to_all x1, blocking collectives: 13.9 us -> 11.3 us  [local(): lax.all_to_all(partial, 'seq', 0, 0, axis_index_groups=groups, tiled=True)]
    pallas_call x3, Pallas kernels: 3.67 us -> 2.34 us  [vmem_call(): return lambda *args: jax.tree.map(in_vmem, call(*args))]
    ppermute x9, starting transfers between devices: 15.7 us -> 15.2 us  [exchange(): return in_vmem(lax.ppermute(value, 'seq', pairs))]
  transfers between devices with their start and end apart: 9 -> 9, of which waited for: 2 -> 4; matrix products, arithmetic and copies ran while one was open for 0% -> 0% of each run, Pallas kernels for 3% -> 3%
where the time goes in v4:
time: 40.1 us; the launch traced here: 39.8 us
  starting transfers between devices  15.2 us (38%)
  blocking collectives  11.3 us (28%)
  waiting for transfers between devices  7.94 us (20%)
  Pallas kernels  4.09 us (10%)
  between operations  1.33 us (3%)
    ppermute x9, starting transfers between devices, exchange(): return in_vmem(lax.ppermute(value, 'seq', pairs))  15.2 us
    all_to_all x1, blocking collectives, local(): lax.all_to_all(partial, 'seq', 0, 0, axis_index_groups=groups, tiled=True)  11.3 us
    ppermute x9, waiting for transfers between devices, exchange(): return in_vmem(lax.ppermute(value, 'seq', pairs))  7.94 us
    pallas_call x3, Pallas kernels, vmem_call(): return lambda *args: jax.tree.map(in_vmem, call(*args))  2.34 us
    pallas_call x1, Pallas kernels, local(): pl.pallas_call(combine_kernel, out_shape=[struct((rows, model), bf), stru...  0.94 us
    pallas_call x1, Pallas kernels, local(): pl.pallas_call(attend_kernel, out_shape=pltpu.VMEM((parts, out_rows, widt...  0.81 us
  transfers between devices with their start and end apart: 9, of which 4 were waited for; matrix products, arithmetic and copies ran while one was open for 0% of the time, Pallas kernels for 3%

profile of v4, /device:TPU:0, one launch (start us, length us, event | category | flops | bytes accessed | tf_op | source)
XLA Modules:
  0.0 39.8 jit_solution(15390319167434953956)
XLA Ops:
  0.6 1.1 %prep.1 = (bf16[8,1152]{1,0:T(8,128)(2,1)S(1)}, bf16[8,1152]{1,0:T(8,128)(2,1)S(1)}, bf16[8,1152]{1,0:T(8,128)(2,1)S(1)}, bf16[8,1152]{1,0:T(8,128)(2,1)S(1)}) custom-call(s32[8]{0:T(128)} %refs_0_.1, f32[1,128]{1,0:T(1,128)} %constant.2.clone.refs_1_, bf16[8,1536]{1,0:T(8,128)(2,1)} %refs_2_.1, bf16[8,1536]{1,0:T(8,128)(2,1)} %refs_3_.1, ...), custom_call_target="tpu_custom_call" | custom-call | tf_op jit(solution)/shard_map/prep/pallas_call | solution.py:52
  1.7 3.1 %collective-permute-start = (bf16[8,1152]{1,0:T(8,128)(2,1)S(1)}, bf16[8,1152]{1,0:T(8,128)(2,1)S(1)}, u32[]{:S(2)}, u32[]{:S(2)}) collective-permute-start(bf16[8,1152]{1,0:T(8,128)(2,1)S(1)} %get-tuple-element.13), channel_id=1, source_target_pairs={{0,5},{1,4},{2,7},{3,6},{4,1},{5,0},{6,3},{7,2},{8,13},{9,12},{10,... | collective-permute-start | bytes 55304 | tf_op jit(solution)/shard_map/ppermute | solution.py:43
  4.8 0.1 collective-permute-start.1
  4.9 0.5 %collective-permute-start.2 = (bf16[8,1152]{1,0:T(8,128)(2,1)S(1)}, bf16[8,1152]{1,0:T(8,128)(2,1)S(1)}, u32[]{:S(2)}, u32[]{:S(2)}) collective-permute-start(bf16[8,1152]{1,0:T(8,128)(2,1)S(1)} %get-tuple-element.15), channel_id=1, source_target_pairs={{0,1},{1,0},{2,3},{3,2},{4,5},{5,4},{6,7},{7,6},{8,9},{9,8},{10,11... | collective-permute-start | bytes 55304 | tf_op jit(solution)/shard_map/ppermute | solution.py:43
  6.1 1.3 %text.1 = (bf16[128,384]{1,0:T(8,128)(2,1)S(1)}, bf16[128,384]{1,0:T(8,128)(2,1)S(1)}, bf16[128,384]{1,0:T(8,128)(2,1)S(1)}, f32[8,128]{1,0:T(8,128)S(1)}) custom-call(bf16[512,1536]{1,0:T(8,128)(2,1)} %q_h.1, bf16[512,1536]{1,0:T(8,128)(2,1)} %k_h.1, bf16[512,1536]{1,0:T(8,128)(2,1)} %v_h.1, f32[1,128]{1,0:T(1,128)} %bitcast.6, f32[1,128]{1,0:T(1,128)} %bitcast.7, ...), custom_call_target="tpu_custom_call" | custom-call | flops 20000000 | bytes 600000 | tf_op jit(solution)/shard_map/text/pallas_call | solution.py:52
  7.4 0.0 collective-permute-done.a1
  7.4 1.2 %collective-permute-done.1.a2 = bf16[8,1152]{1,0:T(8,128)(2,1)S(1)} collective-permute-done((bf16[8,1152]{1,0:T(8,128)(2,1)S(1)}, bf16[8,1152]{1,0:T(8,128)(2,1)S(1)}, u32[]{:S(2)}, u32[]{:S(2)}) %collective-permute-start.1) | collective-permute-done | bytes 18464 | tf_op jit(solution)/shard_map/ppermute | solution.py:43
  8.6 0.1 collective-permute-done.2.a3
  8.7 2.2 %collective-permute-start.8 = (bf16[32,384]{1,0:T(8,128)(2,1)S(1)}, bf16[32,384]{1,0:T(8,128)(2,1)S(1)}, u32[]{:S(2)}, u32[]{:S(2)}) collective-permute-start(bf16[32,384]{1,0:T(8,128)(2,1)S(1)} %get-tuple-element.18.q0), channel_id=1, source_target_pairs={{0,3},{1,2},{2,1},{3,0},{4,7},{5,6},{6,5},{7,4},{8,11},{9,10},{10,... | collective-permute-start | bytes 73736 | tf_op jit(solution)/shard_map/ppermute | solution.py:43
  10.9 2.8 %collective-permute-start.5 = (bf16[32,768]{1,0:T(8,128)(2,1)S(1)}, bf16[32,768]{1,0:T(8,128)(2,1)S(1)}, u32[]{:S(2)}, u32[]{:S(2)}) collective-permute-start(bf16[32,768]{1,0:T(8,128)(2,1)S(1)} %get-tuple-element.17.kv0), channel_id=1, source_target_pairs={{0,48},{1,49},{2,50},{3,51},{4,52},{5,53},{6,54},{7,55},{8,56},{9,... | collective-permute-start | bytes 147464 | tf_op jit(solution)/shard_map/ppermute | solution.py:43
  13.7 0.2 collective-permute-start.4
  13.9 1.7 %collective-permute-start.3 = (bf16[32,768]{1,0:T(8,128)(2,1)S(1)}, bf16[32,768]{1,0:T(8,128)(2,1)S(1)}, u32[]{:S(2)}, u32[]{:S(2)}) collective-permute-start(bf16[32,768]{1,0:T(8,128)(2,1)S(1)} %get-tuple-element.17.kv0), channel_id=1, source_target_pairs={{0,32},{1,33},{2,34},{3,35},{4,36},{5,37},{6,38},{7,39},{8,40},{9,... | collective-permute-start | bytes 147464 | tf_op jit(solution)/shard_map/ppermute | solution.py:43
  15.6 4.0 %collective-permute-start.7 = (bf16[32,384]{1,0:T(8,128)(2,1)S(1)}, bf16[32,384]{1,0:T(8,128)(2,1)S(1)}, u32[]{:S(2)}, u32[]{:S(2)}) collective-permute-start(bf16[32,384]{1,0:T(8,128)(2,1)S(1)} %get-tuple-element.18.q0), channel_id=1, source_target_pairs={{0,12},{1,13},{2,14},{3,15},{4,8},{5,9},{6,10},{7,11},{8,4},{9,5},... | collective-permute-start | bytes 73736 | tf_op jit(solution)/shard_map/ppermute | solution.py:43
  19.6 0.0 collective-permute-done.8.q3
  19.6 0.5 %collective-permute-start.6 = (bf16[32,384]{1,0:T(8,128)(2,1)S(1)}, bf16[32,384]{1,0:T(8,128)(2,1)S(1)}, u32[]{:S(2)}, u32[]{:S(2)}) collective-permute-start(bf16[32,384]{1,0:T(8,128)(2,1)S(1)} %get-tuple-element.18.q0), channel_id=1, source_target_pairs={{0,15},{1,14},{2,13},{3,12},{4,11},{5,10},{6,9},{7,8},{8,7},{9,6},... | collective-permute-start | bytes 73736 | tf_op jit(solution)/shard_map/ppermute | solution.py:43
  20.1 1.3 %collective-permute-done.7.q2 = bf16[32,384]{1,0:T(8,128)(2,1)S(1)} collective-permute-done((bf16[32,384]{1,0:T(8,128)(2,1)S(1)}, bf16[32,384]{1,0:T(8,128)(2,1)S(1)}, u32[]{:S(2)}, u32[]{:S(2)}) %collective-permute-start.7) | collective-permute-done | bytes 24608 | tf_op jit(solution)/shard_map/ppermute | solution.py:43
  21.4 5.3 %collective-permute-done.6.q1 = bf16[32,384]{1,0:T(8,128)(2,1)S(1)} collective-permute-done((bf16[32,384]{1,0:T(8,128)(2,1)S(1)}, bf16[32,384]{1,0:T(8,128)(2,1)S(1)}, u32[]{:S(2)}, u32[]{:S(2)}) %collective-permute-start.6) | collective-permute-done | bytes 24608 | tf_op jit(solution)/shard_map/ppermute | solution.py:43
  26.8 0.0 collective-permute-done.5.kv3
  26.8 0.0 collective-permute-done.4.kv2
  26.8 0.0 collective-permute-done.3.kv1
  26.8 0.8 %attend.1 = bf16[16,16,512]{2,1,0:T(8,128)(2,1)S(1)} custom-call(bf16[32,768]{1,0:T(8,128)(2,1)S(1)} %get-tuple-element.17.kv0, bf16[32,768]{1,0:T(8,128)(2,1)S(1)} %collective-permute-done.3.kv1, bf16[32,768]{1,0:T(8,128)(2,1)S(1)} %collective-permute-done.4.kv2, bf16[32,768]{1,0:T(8,128)(2,1)S(1)} %collective-permute-done.5.kv3, ...), custom_call_target="tpu_custom_call" | custom-call | tf_op jit(solution)/shard_map/attend/pallas_call | solution.py:301
  27.6 11.3 %all_to_all.5.got = bf16[16,16,512]{2,1,0:T(8,128)(2,1)S(1)} all-to-all(bf16[16,16,512]{2,1,0:T(8,128)(2,1)S(1)} %attend.1), channel_id=1, replica_groups={{0,1,2,3,4,5,6,7,8,9,10,11,12,13,14,15},{16,17,18,19,20,21,22,23,24,25,..., dimensions={0} | all-to-all | bytes 524288 | tf_op jit(solution)/shard_map/all_to_all | solution.py:310
  38.9 0.9 %combine.1 = (bf16[8,1536]{1,0:T(8,128)(2,1)}, bf16[8,1536]{1,0:T(8,128)(2,1)}) custom-call(bf16[16,16,512]{2,1,0:T(8,128)(2,1)S(1)} %all_to_all.5.got), custom_call_target="tpu_custom_call" | custom-call | tf_op jit(solution)/shard_map/combine/pallas_call | solution.py:312
  (1 shorter events, 0.0 us)
Async XLA Ops:
  1.7 5.7 %collective-permute-start = (bf16[8,1152]{1,0:T(8,128)(2,1)S(1)}, bf16[8,1152]{1,0:T(8,128)(2,1)S(1)}, u32[]{:S(2)}, u32[]{:S(2)}) collective-permute-start(bf16[8,1152]{1,0:T(8,128)(2,1)S(1)} %get-tuple-element.13), channel_id=1, source_target_pairs={{0,5},{1,4},{2,7},{3,6},{4,1},{5,0},{6,3},{7,2},{8,13},{9,12},{10,... | collective-permute-start | bytes 55304 | tf_op jit(solution)/shard_map/ppermute | solution.py:43
  4.8 3.8 %collective-permute-start.1 = (bf16[8,1152]{1,0:T(8,128)(2,1)S(1)}, bf16[8,1152]{1,0:T(8,128)(2,1)S(1)}, u32[]{:S(2)}, u32[]{:S(2)}) collective-permute-start(bf16[8,1152]{1,0:T(8,128)(2,1)S(1)} %get-tuple-element.14), channel_id=1, source_target_pairs={{0,4},{1,5},{2,6},{3,7},{4,0},{5,1},{6,2},{7,3},{8,12},{9,13},{10,... | collective-permute-start | bytes 55304 | tf_op jit(solution)/shard_map/ppermute | solution.py:43
  4.9 3.8 %collective-permute-start.2 = (bf16[8,1152]{1,0:T(8,128)(2,1)S(1)}, bf16[8,1152]{1,0:T(8,128)(2,1)S(1)}, u32[]{:S(2)}, u32[]{:S(2)}) collective-permute-start(bf16[8,1152]{1,0:T(8,128)(2,1)S(1)} %get-tuple-element.15), channel_id=1, source_target_pairs={{0,1},{1,0},{2,3},{3,2},{4,5},{5,4},{6,7},{7,6},{8,9},{9,8},{10,11... | collective-permute-start | bytes 55304 | tf_op jit(solution)/shard_map/ppermute | solution.py:43
  8.7 10.9 %collective-permute-start.8 = (bf16[32,384]{1,0:T(8,128)(2,1)S(1)}, bf16[32,384]{1,0:T(8,128)(2,1)S(1)}, u32[]{:S(2)}, u32[]{:S(2)}) collective-permute-start(bf16[32,384]{1,0:T(8,128)(2,1)S(1)} %get-tuple-element.18.q0), channel_id=1, source_target_pairs={{0,3},{1,2},{2,1},{3,0},{4,7},{5,6},{6,5},{7,4},{8,11},{9,10},{10,... | collective-permute-start | bytes 73736 | tf_op jit(solution)/shard_map/ppermute | solution.py:43
  10.9 15.8 %collective-permute-start.5 = (bf16[32,768]{1,0:T(8,128)(2,1)S(1)}, bf16[32,768]{1,0:T(8,128)(2,1)S(1)}, u32[]{:S(2)}, u32[]{:S(2)}) collective-permute-start(bf16[32,768]{1,0:T(8,128)(2,1)S(1)} %get-tuple-element.17.kv0), channel_id=1, source_target_pairs={{0,48},{1,49},{2,50},{3,51},{4,52},{5,53},{6,54},{7,55},{8,56},{9,... | collective-permute-start | bytes 147464 | tf_op jit(solution)/shard_map/ppermute | solution.py:43
  13.7 13.1 %collective-permute-start.4 = (bf16[32,768]{1,0:T(8,128)(2,1)S(1)}, bf16[32,768]{1,0:T(8,128)(2,1)S(1)}, u32[]{:S(2)}, u32[]{:S(2)}) collective-permute-start(bf16[32,768]{1,0:T(8,128)(2,1)S(1)} %get-tuple-element.17.kv0), channel_id=1, source_target_pairs={{0,16},{1,17},{2,18},{3,19},{4,20},{5,21},{6,22},{7,23},{8,24},{9,... | collective-permute-start | bytes 147464 | tf_op jit(solution)/shard_map/ppermute | solution.py:43
  13.9 12.9 %collective-permute-start.3 = (bf16[32,768]{1,0:T(8,128)(2,1)S(1)}, bf16[32,768]{1,0:T(8,128)(2,1)S(1)}, u32[]{:S(2)}, u32[]{:S(2)}) collective-permute-start(bf16[32,768]{1,0:T(8,128)(2,1)S(1)} %get-tuple-element.17.kv0), channel_id=1, source_target_pairs={{0,32},{1,33},{2,34},{3,35},{4,36},{5,37},{6,38},{7,39},{8,40},{9,... | collective-permute-start | bytes 147464 | tf_op jit(solution)/shard_map/ppermute | solution.py:43
  15.6 5.8 %collective-permute-start.7 = (bf16[32,384]{1,0:T(8,128)(2,1)S(1)}, bf16[32,384]{1,0:T(8,128)(2,1)S(1)}, u32[]{:S(2)}, u32[]{:S(2)}) collective-permute-start(bf16[32,384]{1,0:T(8,128)(2,1)S(1)} %get-tuple-element.18.q0), channel_id=1, source_target_pairs={{0,12},{1,13},{2,14},{3,15},{4,8},{5,9},{6,10},{7,11},{8,4},{9,5},... | collective-permute-start | bytes 73736 | tf_op jit(solution)/shard_map/ppermute | solution.py:43
  19.6 7.1 %collective-permute-start.6 = (bf16[32,384]{1,0:T(8,128)(2,1)S(1)}, bf16[32,384]{1,0:T(8,128)(2,1)S(1)}, u32[]{:S(2)}, u32[]{:S(2)}) collective-permute-start(bf16[32,384]{1,0:T(8,128)(2,1)S(1)} %get-tuple-element.18.q0), channel_id=1, source_target_pairs={{0,15},{1,14},{2,13},{3,12},{4,11},{5,10},{6,9},{7,8},{8,7},{9,6},... | collective-permute-start | bytes 73736 | tf_op jit(solution)/shard_map/ppermute | solution.py:43

commit v5 on v4

--- a/solution.py
+++ b/solution.py
@@ -31,8 +31,8 @@
 
 
 HEAD_STEPS = ((0, 0, 0), (0, 1, 1), (0, 1, 0), (0, 0, 1))
-QUERY_STEPS = ((0, 0, 0), (0, 3, 3), (0, 3, 0), (0, 0, 3))
-KEY_STEPS = ((0, 0, 0), (2, 0, 0), (1, 0, 0), (3, 0, 0))
+QUERY_STEPS = ((0, 0, 0), (0, 3, 0), (0, 0, 3), (0, 3, 3))
+KEY_STEPS = ((0, 0, 0), (1, 0, 0), (3, 0, 0), (2, 0, 0))
 
 
 def exchange(value, step):
@@ -123,6 +123,12 @@
         q[j * rows : (j + 1) * rows, :] = a[:, 2 * width :]
 
 
+def join_kernel(a, b, out):
+    rows = a.shape[0]
+    out[:rows, :] = a[...]
+    out[rows:, :] = b[...]
+
+
 def text_kernel(q_h, k_h, v_h, qg_h, kg_h, length_h, q_out, k_out, v_out, bias, length, q_in, k_in, qg, kg, sems):
     block, width = q_in.shape
     x, z, y = split_index(lax.axis_index("seq"))
@@ -150,12 +156,12 @@
     bias[...] = jnp.where(key < length[0], 0.0, MASKED)
 
 
-def attend_kernel(kv0, kv1, kv2, kv3, q0, q1, q2, q3, qt, kt, vt, bias, out):
-    kvs, qs = (kv0, kv1, kv2, kv3), (q0, q1, q2, q3)
+def attend_kernel(kv0, kv1, q0, q1, qt, kt, vt, bias, out):
+    kvs, qs = (kv0, kv1), (q0, q1)
     width = qt.shape[1]
     heads = width // HD
     text_keys = kt.shape[0]
-    image_rows = SIDE * q0.shape[0]
+    image_rows = 2 * q0.shape[0]
     rows = image_rows + qt.shape[0]
     _, z, y = split_index(lax.axis_index("seq"))
     masked = bias[0:1, :]
@@ -293,18 +299,31 @@
         name="pack",
     )(*from_y, bias)
 
-    kvs = [kv] + [exchange(kv, step) for step in KEY_STEPS[1:]]
-    qs = [q] + [exchange(q, step) for step in QUERY_STEPS[1:]]
+    def join(a, b):
+        return vmem_call(
+            join_kernel,
+            out_shape=pltpu.VMEM((a.shape[0] + b.shape[0], a.shape[1]), a.dtype),
+            in_specs=[VM] * 2,
+            out_specs=VM,
+            name="join",
+        )(a, b)
+
+    kv_next = exchange(kv, KEY_STEPS[1])
+    q_next = exchange(q, QUERY_STEPS[1])
+    kv_two = join(kv, kv_next)
+    kv_last = exchange(kv_two, KEY_STEPS[2])
+    q_two = join(q, q_next)
+    q_last = exchange(q_two, QUERY_STEPS[2])
 
     parts = SIDE * SIDE
     out_rows = rows + text_rows // SIDE**3
     partial = pl.pallas_call(
         attend_kernel,
         out_shape=pltpu.VMEM((parts, out_rows, width + HD), bf),
-        in_specs=[VM] * 12,
+        in_specs=[VM] * 8,
         out_specs=VM,
         name="attend",
-    )(*kvs, *qs, qt, kt, vt, bias)
+    )(kv_two, kv_last, q_two, q_last, qt, kt, vt, bias)
 
     groups = [[x * parts + i for i in range(parts)] for x in range(SIDE)]
     got = in_vmem(lax.all_to_all(partial, "seq", 0, 0, axis_index_groups=groups, tiled=True))
@@ -318,11 +337,15 @@
     )(got)
 
 
+def whole(*args):
+    return tuple(local(*args))
+
+
 def solution(mesh):
     token = P(("req", "seq"), None)
     text = P("req", None)
     return jax.shard_map(
-        lambda *args: tuple(local(*args)),
+        whole,
         mesh=mesh,
         in_specs=(token, token, token, text, text, text, P(), P(), P(), P(), P(("req", "seq")), P("req")),
         out_specs=(token, token),

time: 40.1 us -> 43.5 us (1.085)
  blocking collectives: 11.3 us -> 14.7 us
  starting transfers between devices: 15.2 us -> 14.3 us
  waiting for transfers between devices: 7.94 us -> 8.8 us
    all_to_all x1, blocking collectives: 11.3 us -> 14.7 us  [local(): lax.all_to_all(partial, 'seq', 0, 0, axis_index_groups=groups, tiled=True)]
    ppermute x9 -> x7, starting transfers between devices: 15.2 us -> 14.3 us  [exchange(): return in_vmem(lax.ppermute(value, 'seq', pairs))]
    ppermute x9 -> x7, waiting for transfers between devices: 7.94 us -> 8.8 us  [exchange(): return in_vmem(lax.ppermute(value, 'seq', pairs))]
    pallas_call x3 -> x5, Pallas kernels: 2.34 us -> 2.36 us  [vmem_call(): return lambda *args: jax.tree.map(in_vmem, call(*args))]
  transfers between devices with their start and end apart: 9 -> 7, of which waited for: 4 -> 5; matrix products, arithmetic and copies ran while one was open for 0% -> 0% of each run, Pallas kernels for 3% -> 3%
where the time goes in v5:
time: 43.5 us; the launch traced here: 43.3 us
  blocking collectives  14.7 us (34%)
  starting transfers between devices  14.3 us (33%)
  waiting for transfers between devices  8.8 us (20%)
  Pallas kernels  4.1 us (9%)
  between operations  1.33 us (3%)
    all_to_all x1, blocking collectives, local(): lax.all_to_all(partial, 'seq', 0, 0, axis_index_groups=groups, tiled=True)  14.7 us
    ppermute x7, starting transfers between devices, exchange(): return in_vmem(lax.ppermute(value, 'seq', pairs))  14.3 us
    ppermute x7, waiting for transfers between devices, exchange(): return in_vmem(lax.ppermute(value, 'seq', pairs))  8.8 us
    pallas_call x5, Pallas kernels, vmem_call(): return lambda *args: jax.tree.map(in_vmem, call(*args))  2.36 us
    pallas_call x1, Pallas kernels, local(): pl.pallas_call(combine_kernel, out_shape=[struct((rows, model), bf), stru...  0.94 us
  transfers between devices with their start and end apart: 7, of which 5 were waited for; matrix products, arithmetic and copies ran while one was open for 0% of the time, Pallas kernels for 3%

profile of v5, /device:TPU:0, one launch (start us, length us, event | category | flops | bytes accessed | tf_op | source)
XLA Modules:
  0.0 43.3 jit_solution(16524296262764498459)
XLA Ops:
  0.6 1.1 %prep.1 = (bf16[8,1152]{1,0:T(8,128)(2,1)S(1)}, bf16[8,1152]{1,0:T(8,128)(2,1)S(1)}, bf16[8,1152]{1,0:T(8,128)(2,1)S(1)}, bf16[8,1152]{1,0:T(8,128)(2,1)S(1)}) custom-call(s32[8]{0:T(128)} %refs_0_.1, f32[1,128]{1,0:T(1,128)} %constant.2.clone.refs_1_, bf16[8,1536]{1,0:T(8,128)(2,1)} %refs_2_.1, bf16[8,1536]{1,0:T(8,128)(2,1)} %refs_3_.1, ...), custom_call_target="tpu_custom_call" | custom-call | tf_op jit(solution)/shard_map/prep/pallas_call | solution.py:52
  1.7 3.1 %collective-permute-start = (bf16[8,1152]{1,0:T(8,128)(2,1)S(1)}, bf16[8,1152]{1,0:T(8,128)(2,1)S(1)}, u32[]{:S(2)}, u32[]{:S(2)}) collective-permute-start(bf16[8,1152]{1,0:T(8,128)(2,1)S(1)} %get-tuple-element.13), channel_id=1, source_target_pairs={{0,5},{1,4},{2,7},{3,6},{4,1},{5,0},{6,3},{7,2},{8,13},{9,12},{10,... | collective-permute-start | bytes 55304 | tf_op jit(solution)/shard_map/ppermute | solution.py:43
  4.8 0.1 collective-permute-start.1
  4.9 0.5 %collective-permute-start.2 = (bf16[8,1152]{1,0:T(8,128)(2,1)S(1)}, bf16[8,1152]{1,0:T(8,128)(2,1)S(1)}, u32[]{:S(2)}, u32[]{:S(2)}) collective-permute-start(bf16[8,1152]{1,0:T(8,128)(2,1)S(1)} %get-tuple-element.15), channel_id=1, source_target_pairs={{0,1},{1,0},{2,3},{3,2},{4,5},{5,4},{6,7},{7,6},{8,9},{9,8},{10,11... | collective-permute-start | bytes 55304 | tf_op jit(solution)/shard_map/ppermute | solution.py:43
  6.1 1.3 %text.1 = (bf16[128,384]{1,0:T(8,128)(2,1)S(1)}, bf16[128,384]{1,0:T(8,128)(2,1)S(1)}, bf16[128,384]{1,0:T(8,128)(2,1)S(1)}, f32[8,128]{1,0:T(8,128)S(1)}) custom-call(bf16[512,1536]{1,0:T(8,128)(2,1)} %q_h.1, bf16[512,1536]{1,0:T(8,128)(2,1)} %k_h.1, bf16[512,1536]{1,0:T(8,128)(2,1)} %v_h.1, f32[1,128]{1,0:T(1,128)} %bitcast.6, f32[1,128]{1,0:T(1,128)} %bitcast.7, ...), custom_call_target="tpu_custom_call" | custom-call | flops 20000000 | bytes 600000 | tf_op jit(solution)/shard_map/text/pallas_call | solution.py:52
  7.4 0.0 collective-permute-done.a1
  7.4 1.2 %collective-permute-done.1.a2 = bf16[8,1152]{1,0:T(8,128)(2,1)S(1)} collective-permute-done((bf16[8,1152]{1,0:T(8,128)(2,1)S(1)}, bf16[8,1152]{1,0:T(8,128)(2,1)S(1)}, u32[]{:S(2)}, u32[]{:S(2)}) %collective-permute-start.1) | collective-permute-done | bytes 18464 | tf_op jit(solution)/shard_map/ppermute | solution.py:43
  8.6 0.1 collective-permute-done.2.a3
  8.7 1.5 %collective-permute-start.3 = (bf16[32,768]{1,0:T(8,128)(2,1)S(1)}, bf16[32,768]{1,0:T(8,128)(2,1)S(1)}, u32[]{:S(2)}, u32[]{:S(2)}) collective-permute-start(bf16[32,768]{1,0:T(8,128)(2,1)S(1)} %get-tuple-element.17.a), channel_id=1, source_target_pairs={{0,16},{1,17},{2,18},{3,19},{4,20},{5,21},{6,22},{7,23},{8,24},{9,... | collective-permute-start | bytes 147464 | tf_op jit(solution)/shard_map/ppermute | solution.py:43
  10.3 2.6 %collective-permute-done.3.b = bf16[32,768]{1,0:T(8,128)(2,1)S(1)} collective-permute-done((bf16[32,768]{1,0:T(8,128)(2,1)S(1)}, bf16[32,768]{1,0:T(8,128)(2,1)S(1)}, u32[]{:S(2)}, u32[]{:S(2)}) %collective-permute-start.3) | collective-permute-done | bytes 49184 | tf_op jit(solution)/shard_map/ppermute | solution.py:43
  12.9 2.8 %collective-permute-start.4 = (bf16[64,768]{1,0:T(8,128)(2,1)S(1)}, bf16[64,768]{1,0:T(8,128)(2,1)S(1)}, u32[]{:S(2)}, u32[]{:S(2)}) collective-permute-start(bf16[64,768]{1,0:T(8,128)(2,1)S(1)} %join.2.kv0), channel_id=1, source_target_pairs={{0,48},{1,49},{2,50},{3,51},{4,52},{5,53},{6,54},{7,55},{8,56},{9,... | collective-permute-start | bytes 294920 | tf_op jit(solution)/shard_map/ppermute | solution.py:43
  15.7 4.0 %collective-permute-start.5 = (bf16[32,384]{1,0:T(8,128)(2,1)S(1)}, bf16[32,384]{1,0:T(8,128)(2,1)S(1)}, u32[]{:S(2)}, u32[]{:S(2)}) collective-permute-start(bf16[32,384]{1,0:T(8,128)(2,1)S(1)} %get-tuple-element.18.a), channel_id=1, source_target_pairs={{0,12},{1,13},{2,14},{3,15},{4,8},{5,9},{6,10},{7,11},{8,4},{9,5},... | collective-permute-start | bytes 73736 | tf_op jit(solution)/shard_map/ppermute | solution.py:43
  19.7 1.8 %collective-permute-done.5.b = bf16[32,384]{1,0:T(8,128)(2,1)S(1)} collective-permute-done((bf16[32,384]{1,0:T(8,128)(2,1)S(1)}, bf16[32,384]{1,0:T(8,128)(2,1)S(1)}, u32[]{:S(2)}, u32[]{:S(2)}) %collective-permute-start.5) | collective-permute-done | bytes 24608 | tf_op jit(solution)/shard_map/ppermute | solution.py:43
  21.5 2.2 %collective-permute-start.6 = (bf16[64,384]{1,0:T(8,128)(2,1)S(1)}, bf16[64,384]{1,0:T(8,128)(2,1)S(1)}, u32[]{:S(2)}, u32[]{:S(2)}) collective-permute-start(bf16[64,384]{1,0:T(8,128)(2,1)S(1)} %join.3.q0), channel_id=1, source_target_pairs={{0,3},{1,2},{2,1},{3,0},{4,7},{5,6},{6,5},{7,4},{8,11},{9,10},{10,... | collective-permute-start | bytes 147464 | tf_op jit(solution)/shard_map/ppermute | solution.py:43
  23.7 3.1 %collective-permute-done.6.q1 = bf16[64,384]{1,0:T(8,128)(2,1)S(1)} collective-permute-done((bf16[64,384]{1,0:T(8,128)(2,1)S(1)}, bf16[64,384]{1,0:T(8,128)(2,1)S(1)}, u32[]{:S(2)}, u32[]{:S(2)}) %collective-permute-start.6) | collective-permute-done | bytes 49184 | tf_op jit(solution)/shard_map/ppermute | solution.py:43
  26.8 0.0 collective-permute-done.4.kv1
  26.8 0.8 %attend.1 = bf16[16,16,512]{2,1,0:T(8,128)(2,1)S(1)} custom-call(bf16[64,768]{1,0:T(8,128)(2,1)S(1)} %join.2.kv0, bf16[64,768]{1,0:T(8,128)(2,1)S(1)} %collective-permute-done.4.kv1, bf16[64,384]{1,0:T(8,128)(2,1)S(1)} %join.3.q0, bf16[64,384]{1,0:T(8,128)(2,1)S(1)} %collective-permute-done.6.q1, bf16[128,384]{1,0:T(8,128)(2,1)S(1)} %get-tuple-element.19.qt, ...), custom_call_target="tpu_custom_call" | custom-call | tf_op jit(solution)/shard_map/attend/pallas_call | solution.py:320
  27.6 14.7 %all_to_all.5.got = bf16[16,16,512]{2,1,0:T(8,128)(2,1)S(1)} all-to-all(bf16[16,16,512]{2,1,0:T(8,128)(2,1)S(1)} %attend.1), channel_id=1, replica_groups={{0,1,2,3,4,5,6,7,8,9,10,11,12,13,14,15},{16,17,18,19,20,21,22,23,24,25,..., dimensions={0} | all-to-all | bytes 524288 | tf_op jit(solution)/shard_map/all_to_all | solution.py:329
  42.3 0.9 %combine.1 = (bf16[8,1536]{1,0:T(8,128)(2,1)}, bf16[8,1536]{1,0:T(8,128)(2,1)}) custom-call(bf16[16,16,512]{2,1,0:T(8,128)(2,1)S(1)} %all_to_all.5.got), custom_call_target="tpu_custom_call" | custom-call | tf_op jit(solution)/shard_map/combine/pallas_call | solution.py:331
  (3 shorter events, 0.0 us)
Async XLA Ops:
  1.7 5.7 %collective-permute-start = (bf16[8,1152]{1,0:T(8,128)(2,1)S(1)}, bf16[8,1152]{1,0:T(8,128)(2,1)S(1)}, u32[]{:S(2)}, u32[]{:S(2)}) collective-permute-start(bf16[8,1152]{1,0:T(8,128)(2,1)S(1)} %get-tuple-element.13), channel_id=1, source_target_pairs={{0,5},{1,4},{2,7},{3,6},{4,1},{5,0},{6,3},{7,2},{8,13},{9,12},{10,... | collective-permute-start | bytes 55304 | tf_op jit(solution)/shard_map/ppermute | solution.py:43
  4.8 3.8 %collective-permute-start.1 = (bf16[8,1152]{1,0:T(8,128)(2,1)S(1)}, bf16[8,1152]{1,0:T(8,128)(2,1)S(1)}, u32[]{:S(2)}, u32[]{:S(2)}) collective-permute-start(bf16[8,1152]{1,0:T(8,128)(2,1)S(1)} %get-tuple-element.14), channel_id=1, source_target_pairs={{0,4},{1,5},{2,6},{3,7},{4,0},{5,1},{6,2},{7,3},{8,12},{9,13},{10,... | collective-permute-start | bytes 55304 | tf_op jit(solution)/shard_map/ppermute | solution.py:43
  4.9 3.8 %collective-permute-start.2 = (bf16[8,1152]{1,0:T(8,128)(2,1)S(1)}, bf16[8,1152]{1,0:T(8,128)(2,1)S(1)}, u32[]{:S(2)}, u32[]{:S(2)}) collective-permute-start(bf16[8,1152]{1,0:T(8,128)(2,1)S(1)} %get-tuple-element.15), channel_id=1, source_target_pairs={{0,1},{1,0},{2,3},{3,2},{4,5},{5,4},{6,7},{7,6},{8,9},{9,8},{10,11... | collective-permute-start | bytes 55304 | tf_op jit(solution)/shard_map/ppermute | solution.py:43
  8.7 4.1 %collective-permute-start.3 = (bf16[32,768]{1,0:T(8,128)(2,1)S(1)}, bf16[32,768]{1,0:T(8,128)(2,1)S(1)}, u32[]{:S(2)}, u32[]{:S(2)}) collective-permute-start(bf16[32,768]{1,0:T(8,128)(2,1)S(1)} %get-tuple-element.17.a), channel_id=1, source_target_pairs={{0,16},{1,17},{2,18},{3,19},{4,20},{5,21},{6,22},{7,23},{8,24},{9,... | collective-permute-start | bytes 147464 | tf_op jit(solution)/shard_map/ppermute | solution.py:43
  12.9 13.9 %collective-permute-start.4 = (bf16[64,768]{1,0:T(8,128)(2,1)S(1)}, bf16[64,768]{1,0:T(8,128)(2,1)S(1)}, u32[]{:S(2)}, u32[]{:S(2)}) collective-permute-start(bf16[64,768]{1,0:T(8,128)(2,1)S(1)} %join.2.kv0), channel_id=1, source_target_pairs={{0,48},{1,49},{2,50},{3,51},{4,52},{5,53},{6,54},{7,55},{8,56},{9,... | collective-permute-start | bytes 294920 | tf_op jit(solution)/shard_map/ppermute | solution.py:43
  15.7 5.8 %collective-permute-start.5 = (bf16[32,384]{1,0:T(8,128)(2,1)S(1)}, bf16[32,384]{1,0:T(8,128)(2,1)S(1)}, u32[]{:S(2)}, u32[]{:S(2)}) collective-permute-start(bf16[32,384]{1,0:T(8,128)(2,1)S(1)} %get-tuple-element.18.a), channel_id=1, source_target_pairs={{0,12},{1,13},{2,14},{3,15},{4,8},{5,9},{6,10},{7,11},{8,4},{9,5},... | collective-permute-start | bytes 73736 | tf_op jit(solution)/shard_map/ppermute | solution.py:43
  21.5 5.3 %collective-permute-start.6 = (bf16[64,384]{1,0:T(8,128)(2,1)S(1)}, bf16[64,384]{1,0:T(8,128)(2,1)S(1)}, u32[]{:S(2)}, u32[]{:S(2)}) collective-permute-start(bf16[64,384]{1,0:T(8,128)(2,1)S(1)} %join.3.q0), channel_id=1, source_target_pairs={{0,3},{1,2},{2,1},{3,0},{4,7},{5,6},{6,5},{7,4},{8,11},{9,10},{10,... | collective-permute-start | bytes 147464 | tf_op jit(solution)/shard_map/ppermute | solution.py:43
